TPU v7x, 256 devices: a whole 4x4x8 slice. The times are simulated.
256 devices in a mesh: ep: 16 (over z, core), fsdp: 4 (over x), tp: 4 (over y).
Axes of the slice: x: 4, y: 4, z: 8, core: 2. Of those that a mesh axis runs over, the one named last changes fastest.
Arguments:
- out_grad: bfloat16 [8192, 4096], P(('ep', 'fsdp')), may hold values from -1.5 to 1.5
- routes: int32 [8192, 2], P(('ep', 'fsdp')), may hold values from 0 to 15, all different within a row; in each aligned block of 128 rows (0 to 127, 128 to 255, ...) at most 32 rows name the same one
- chosen_logits: float32 [8192, 2], P(('ep', 'fsdp')), may hold values from -4 to 4
- routed_inputs: bfloat16 [16, 16, 4, 32, 4096], P('ep', None, 'fsdp'), may hold values from -6 to 6
- w_gate: bfloat16 [16, 4096, 1024], P('ep', 'fsdp', 'tp'), may hold values from -0.09375 to 0.09375
- w_up: bfloat16 [16, 4096, 1024], P('ep', 'fsdp', 'tp'), may hold values from -0.09375 to 0.09375
- w_down: bfloat16 [16, 1024, 4096], P('ep', 'tp', 'fsdp'), may hold values from -0.1875 to 0.1875
Outputs:
- input_grad: bfloat16 [8192, 4096], P(('ep', 'fsdp'))
- logit_grad: float32 [8192, 2], P(('ep', 'fsdp'))
- grad_gate: float32 [16, 4096, 1024], P('ep', 'fsdp', 'tp')
- grad_up: float32 [16, 4096, 1024], P('ep', 'fsdp', 'tp')
- grad_down: float32 [16, 1024, 4096], P('ep', 'tp', 'fsdp')
Inputs may be any that keep to these rules, and one draw needn't show every extreme that they name: Each row of routes names 2 different experts. In each token group of 128 consecutive rows no expert is named by more than 32 rows, a bound that some block reaches.
All inputs are finite; a program needn't handle non-finite values.
Results may differ from a plain program's by a relative error of at most 0.015.
Values may be sent and summed in bfloat16 or wider, within the bound.
No kernel may reach another device: no remote copies, remote signals or barrier semaphores. Data moves between devices by JAX's collectives and lax.ppermute only.
A program may use at most 128 MiB of HBM per device.

v0:
```python
import jax
import jax.numpy as jnp
from jax import lax
from jax.sharding import PartitionSpec as P


def laid_out(parts, dim):
    shape = list(parts.shape[1:])
    shape[dim] *= parts.shape[0]
    return jnp.moveaxis(parts, 0, dim).reshape(shape)


def gather_together(arrays, axis, dims):
    ravelled = jnp.concatenate([a.reshape(-1) for a in arrays])
    lines, at, outs = lax.all_gather(ravelled, axis), 0, []
    for a, dim in zip(arrays, dims):
        parts = lines[:, at : at + a.size].reshape(-1, *a.shape)
        outs.append(laid_out(parts, dim))
        at += a.size
    return tuple(outs)


def own_rows(product, width, axis):
    whole = product(jnp.int32(0), width * lax.axis_size(axis)).astype(jnp.bfloat16)
    return lax.psum_scatter(whole, axis, scatter_dimension=0, tiled=True).astype(jnp.float32)


def slot_places(routes, experts, capacity):
    flat_routes = routes.reshape(-1)
    onehot = (flat_routes[:, None] == jnp.arange(experts, dtype=jnp.int32)[None, :]).astype(
        jnp.int32
    )
    earlier = (jnp.cumsum(onehot, axis=0) - onehot).astype(jnp.int32)
    position = jnp.sum(earlier * onehot, axis=1).astype(jnp.int32)
    return (flat_routes * capacity + position).astype(jnp.int32)


def weighted_rows(grad_rows, gate_probs):
    scaled = gate_probs[:, :, None] * grad_rows.astype(jnp.float32)[:, None, :]
    return scaled.astype(jnp.bfloat16).reshape(-1, grad_rows.shape[1])


def fill_slots(values, slot_index, total_slots):
    row_total = values.shape[0]
    source = jnp.full((total_slots,), row_total, jnp.int32)
    source = source.at[slot_index].set(jnp.arange(row_total, dtype=jnp.int32))
    padded = jnp.concatenate([values, jnp.zeros((1, values.shape[1]), values.dtype)], axis=0)
    return jnp.take(padded, source, axis=0)


def combine(returned, slot_index, tokens, per_token):
    picked = jnp.take(returned, slot_index, axis=0).astype(jnp.float32)
    return jnp.sum(picked.reshape(tokens, per_token, -1), axis=1).astype(jnp.bfloat16)


def transpose_dot(left, right):
    return lax.dot_general(
        left, right, (((0,), (0,)), ((), ())), preferred_element_type=jnp.float32
    )


def contract_last(left, right):
    return lax.dot_general(
        left, right, (((1,), (1,)), ((), ())), preferred_element_type=jnp.float32
    )


def on_device(out_grad, routes, chosen_logits, routed_inputs, w_gate, w_up, w_down):
    experts = lax.axis_size("ep")
    tp_count = lax.axis_size("tp")
    tokens, model_width = out_grad.shape
    per_token = routes.shape[1]
    capacity = routed_inputs.shape[3]
    gate_probs = jax.nn.softmax(chosen_logits, axis=-1)
    slot_index = slot_places(routes, experts, capacity)
    inputs = routed_inputs.reshape(-1, model_width)
    narrow = model_width // tp_count
    column_piece = lax.dynamic_slice_in_dim(out_grad, lax.axis_index("tp") * narrow, narrow, 1)
    outgoing = fill_slots(weighted_rows(column_piece, gate_probs), slot_index, experts * capacity)
    arrived = lax.all_to_all(
        outgoing.reshape(experts, capacity, narrow), "ep", split_axis=0, concat_axis=0, tiled=True
    )
    scaled = lax.all_gather(arrived.reshape(-1, narrow), "tp", axis=1, tiled=True)
    gate_full, up_full, down_full = gather_together((w_gate, w_up, w_down), "fsdp", (1, 1, 2))
    gate_full = gate_full[0]
    up_full = up_full[0]
    down_full = down_full[0]
    gate_act = jnp.dot(inputs, gate_full, preferred_element_type=jnp.float32)
    up_act = jnp.dot(inputs, up_full, preferred_element_type=jnp.float32)
    sigmoid_gate = jax.nn.sigmoid(gate_act)
    silu_gate = gate_act * sigmoid_gate
    hidden = (silu_gate * up_act).astype(jnp.bfloat16)
    hidden_grad = contract_last(scaled, down_full)
    products = jnp.sum(hidden_grad * hidden.astype(jnp.float32), axis=1)
    up_grad = (hidden_grad * silu_gate).astype(jnp.bfloat16)
    gate_grad = (
        hidden_grad * up_act * sigmoid_gate * (1.0 + gate_act * (1.0 - sigmoid_gate))
    ).astype(jnp.bfloat16)
    slot_part = contract_last(gate_grad, gate_full) + contract_last(up_grad, up_full)
    pair_grads = jnp.concatenate([gate_grad, up_grad], axis=1)

    def grad_term(first_row, row_count):
        input_cols = lax.dynamic_slice_in_dim(inputs, first_row, row_count, 1)
        scaled_cols = lax.dynamic_slice_in_dim(scaled, first_row, row_count, 1)
        gate_up_part = transpose_dot(input_cols, pair_grads)
        down_part = transpose_dot(scaled_cols, hidden)
        return jnp.concatenate([gate_up_part, down_part], axis=1)

    grad_rows = own_rows(grad_term, model_width // lax.axis_size("fsdp"), "fsdp")
    hidden_units = hidden.shape[1]
    grad_gate = grad_rows[:, :hidden_units][None]
    grad_up = grad_rows[:, hidden_units : 2 * hidden_units][None]
    grad_down = grad_rows[:, 2 * hidden_units :].T[None]
    narrow = model_width // tp_count
    column_sum = lax.psum_scatter(
        slot_part.astype(jnp.bfloat16), "tp", scatter_dimension=1, tiled=True
    ).astype(jnp.float32)
    product_sum = lax.psum(products.astype(jnp.bfloat16), "tp").astype(jnp.float32)
    leaving = (
        column_sum.astype(jnp.bfloat16).reshape(experts, capacity, narrow),
        product_sum.astype(jnp.bfloat16).reshape(experts, capacity),
    )
    back_rows, back_products = (
        lax.all_to_all(leaving[0], "ep", split_axis=0, concat_axis=0, tiled=True),
        lax.all_to_all(leaving[1], "ep", split_axis=0, concat_axis=0, tiled=True),
    )
    combined = combine(back_rows.reshape(-1, narrow), slot_index, tokens, per_token)
    input_grad = lax.all_gather(combined, "tp", axis=1, tiled=True)
    chosen = (
        jnp.take(back_products.reshape(-1), slot_index)
        .astype(jnp.float32)
        .reshape(tokens, per_token)
    )
    logit_grad = chosen - gate_probs * jnp.sum(chosen, axis=1, keepdims=True)
    return (input_grad, logit_grad, grad_gate, grad_up, grad_down)


def solution(mesh):
    return jax.shard_map(
        on_device,
        mesh=mesh,
        in_specs=(
            P(("ep", "fsdp"), None),
            P(("ep", "fsdp"), None),
            P(("ep", "fsdp"), None),
            P("ep", None, "fsdp", None, None),
            P("ep", "fsdp", "tp"),
            P("ep", "fsdp", "tp"),
            P("ep", "tp", "fsdp"),
        ),
        out_specs=(
            P(("ep", "fsdp"), None),
            P(("ep", "fsdp"), None),
            P("ep", "fsdp", "tp"),
            P("ep", "fsdp", "tp"),
            P("ep", "tp", "fsdp"),
        ),
        check_vma=False,
    )
```

profile of v0, /device:TPU:1, one launch (start us, length us, event | category | flops | bytes accessed | tf_op | source)
XLA Modules:
  0.0 340.7 jit_solution(7325050296816589945)
XLA Ops:
  18.4 2.1 gather_fusion
  20.6 37.3 %all_to_all.19 = bf16[16,32,1024]{2,1,0:T(8,128)(2,1)} all-to-all(bf16[16,32,1024]{2,1,0:T(8,128)(2,1)S(1)} %broadcast_select_fusion), channel_id=1, replica_groups=mesh['ep'=16,'fsdp'=4,'tp'=4] {'ep'}, dimensions={0} | all-to-all | bytes 2097152 | tf_op jit(solution)/shard_map/all_to_all | solution.py:80
  58.1 26.2 %all-gather.9.cloned.1.call-done = bf16[3145728]{0:T(1024)(128)(2,1)} async-done(((bf16[786432]{0:T(1024)(128)(2,1)}), bf16[3145728]{0:T(1024)(128)(2,1)}) %all-gather.9.cloned.1.call-update) | async-done | bytes 6291472 | tf_op jit(solution)/shard_map/all_gather | solution.py:15
  84.3 7.8 %reshape.171 = bf16[4,786432]{1,0:T(4,128)(2,1)} reshape(bf16[3145728]{0:T(1024)(128)(2,1)} %all-gather.9.cloned.1.call-done) | data formatting | bytes 12582912 | tf_op jit(solution)/shard_map/all_gather | solution.py:15
  92.1 5.4 %fusion.15 = (bf16[4,262144]{1,0:T(4,128)(2,1)}, bf16[4,262144]{1,0:T(4,128)(2,1)S(1)}, bf16[4,262144]{1,0:T(4,128)(2,1)}) fusion(bf16[4,786432]{1,0:T(4,128)(2,1)} %reshape.171), kind=kLoop, calls=%fused_computation.56 | loop fusion | bytes 12582912 | tf_op jit(solution)/shard_map/slice | solution.py:17
  97.5 3.3 squeeze_reshape_transpose_reshape.7
  100.7 3.5 %squeeze_reshape_transpose_reshape.6 = bf16[4096,256]{1,0:T(8,128)(2,1)S(1)} reshape(bf16[4,262144]{1,0:T(4,128)(2,1)} %get-tuple-element.34) | data formatting | bytes 4194304 | tf_op jit(solution)/shard_map/squeeze;reshape;transpose;reshape | solution.py:86
  104.2 3.6 %copy.64 = bf16[1,4,256,1024]{3,2,1,0:T(8,128)(2,1)} copy(bf16[1,4,256,1024]{3,1,2,0:T(4,128)(2,1)} %bitcast.71) | data formatting | bytes 4194304
  107.8 3.9 %copy.52 = bf16[1,256,4,1024]{1,3,2,0:T(8,128)(2,1)} copy(bf16[1,256,4,1024]{3,1,2,0:T(8,128)(2,1)} %bitcast.70) | data formatting | bytes 4194304 | tf_op jit(solution)/shard_map/transpose | solution.py:10
  111.7 4.3 %convolution_bitcast_fusion = f32[512,256]{0,1:T(8,128)S(1)} fusion(bf16[4096,256]{1,0:T(8,128)(2,1)} %squeeze_reshape_transpose_reshape.7, bf16[512,4096]{1,0:T(8,128)(2,1)} %bitcast.85), kind=kOutput, calls=%fused_computation.11 | convolution fusion | flops 1073741824 | bytes 6815744 | tf_op jit(solution)/shard_map/dot_general | solution.py:88
  116.0 2.1 convolution_bitcast_fusion.1
  118.1 19.4 %all-gather.5.cloned.1.call-done = bf16[512,4096]{1,0:T(8,128)(2,1)} async-done(((bf16[512,1024]{1,0:T(8,128)(2,1)}), bf16[512,4096]{1,0:T(8,128)(2,1)}) %all-gather.5.cloned.1.call-update) | async-done | bytes 4194320 | tf_op jit(solution)/shard_map/all_gather | solution.py:83
  137.5 4.5 %multiply_reduce_fusion = (bf16[512]{0:T(512)(128)(2,1)S(1)}, bf16[512,256]{0,1:T(8,128)(2,1)S(1)}, bf16[512,256]{0,1:T(8,128)(2,1)S(1)}, bf16[512,256]{0,1:T(8,128)(2,1)S(1)}) fusion(f32[512,256]{0,1:T(8,128)} %convolution_bitcast_fusion.1, f32[512,256]{0,1:T(8,128)S(1)} %convolution_bitcast_fusion, bf16[512,4096]{1,0:T(8,128)(2,1)} %all-gather.5.cloned.1.call-done, ...), kind=kOutput, calls=%fused_computation.23 | convolution fusion | flops 1076100608 | bytes 8127488 | tf_op jit(solution)/shard_map/dot_general | solution.py:63
  143.4 3.4 add_convert_fusion
  146.9 6.6 %psum.7 = bf16[16,1,32]{2,0,1:T(8,128)(2,1)S(1)} all-reduce(bf16[16,1,32]{2,0,1:T(8,128)(2,1)S(1)} %all_to_all.14), channel_id=1, replica_groups=mesh['ep'=16,'fsdp'=4,'tp'=4] {'tp'}, use_global_device_ids=true, to_apply=%region_9.10 | all-reduce | flops 512 | bytes 2048 | tf_op jit(solution)/shard_map/psum | solution.py:118
  153.5 17.0 %all_to_all.20 = bf16[16,1,32]{2,1,0:T(2,128)(2,1)S(1)} all-to-all(bf16[16,1,32]{2,1,0:T(2,128)(2,1)S(1)} %copy.53), channel_id=1, replica_groups=mesh['ep'=16,'fsdp'=4,'tp'=4] {'ep'}, dimensions={0} | all-to-all | bytes 2048 | tf_op jit(solution)/shard_map/all_to_all | solution.py:125
  170.5 26.2 %reduce-scatter.3.cloned.1.call-done = bf16[512,1024]{1,0:T(8,128)(2,1)} async-done(((bf16[512,4096]{1,0:T(8,128)(2,1)}), bf16[512,1024]{1,0:T(8,128)(2,1)}) %reduce-scatter.3.cloned.1.call-update) | async-done | bytes 1048592 | tf_op jit(solution)/shard_map/reduce_scatter | solution.py:115
  196.7 7.9 %all-to-all-start.1 = ((bf16[16,32,1024]{2,1,0:T(8,128)(2,1)}), bf16[16,32,1024]{2,1,0:T(8,128)(2,1)S(1)}, u32[]{:S(2)}, u32[]{:S(2)}) async-start(bf16[16,32,1024]{2,1,0:T(8,128)(2,1)} %bitcast.78), calls=%async_computation.2 | async-start | bytes 2097152 | tf_op jit(solution)/shard_map/all_to_all | solution.py:124
  207.4 25.3 %all-to-all-done.1 = bf16[16,32,1024]{2,1,0:T(8,128)(2,1)S(1)} async-done(((bf16[16,32,1024]{2,1,0:T(8,128)(2,1)}), bf16[16,32,1024]{2,1,0:T(8,128)(2,1)S(1)}, u32[]{:S(2)}, u32[]{:S(2)}) %all-to-all-start.1) | async-done | bytes 1048608 | tf_op jit(solution)/shard_map/all_to_all | solution.py:124
  236.3 3.7 %convolution_convert_fusion.1 = bf16[4096,256]{0,1:T(8,128)(2,1)S(1)} fusion(bf16[512,256]{0,1:T(8,128)(2,1)S(1)} %get-tuple-element.33, bf16[512,4096]{1,0:T(8,128)(2,1)} %all-gather.5.cloned.1.call-done), kind=kOutput, calls=%fused_computation.8 | convolution fusion | flops 1074790400 | bytes 6553600 | tf_op jit(solution)/shard_map/dot_general | solution.py:57
  240.0 2.4 fusion
  242.4 3.4 %pad_maximum_fusion = bf16[4096,768]{0,1:T(8,128)(2,1)} fusion(bf16[4096,256]{0,1:T(8,128)(2,1)S(1)} %convolution_convert_fusion.1, bf16[4096,512]{0,1:T(8,128)(2,1)S(1)} %fusion), kind=kLoop, calls=%fused_computation.5 | loop fusion | flops 12582912 | bytes 12582912 | tf_op jit(solution)/shard_map/concatenate | solution.py:107
  246.4 9.8 %all-gather.7.cloned.1.call-done = bf16[128,4096]{1,0:T(8,128)(2,1)} async-done(((bf16[128,1024]{1,0:T(8,128)(2,1)}), bf16[128,4096]{1,0:T(8,128)(2,1)}) %all-gather.7.cloned.1.call-update) | async-done | bytes 1048592 | tf_op jit(solution)/shard_map/all_gather | solution.py:128
  256.2 71.4 %reduce-scatter.5.cloned.1.call-done = bf16[1024,768]{0,1:T(8,128)(2,1)} async-done(((bf16[4096,768]{0,1:T(8,128)(2,1)}), bf16[1024,768]{0,1:T(8,128)(2,1)}) %reduce-scatter.5.cloned.1.call-update) | async-done | bytes 1572880 | tf_op jit(solution)/shard_map/reduce_scatter | solution.py:25
  (78 shorter events, 26.3 us)
Async XLA Ops:
  7.2 77.2 %all-gather.9.cloned.1.call-start = ((), (), s32[]{:S(2)}) async-start(), calls=%async_computation.9 | async-start | bytes 7864320 | tf_op jit(solution)/shard_map/all_gather | solution.py:15
  10.1 2.5 copy-start.3
  12.5 2.6 copy-start.2
  12.6 125.0 %all-gather.5.cloned.1.call-start = ((), (), s32[]{:S(2)}) async-start(), calls=%async_computation.5 | async-start | bytes 5242880 | tf_op jit(solution)/shard_map/all_gather | solution.py:83
  57.9 138.8 %reduce-scatter.3.cloned.1.call-start = ((), (), s32[]{:S(2)}) async-start(), calls=%async_computation.6 | async-start | bytes 5242880 | tf_op jit(solution)/shard_map/reduce_scatter | solution.py:115
  111.7 4.3 %copy-start.4 = (bf16[1,16,1,32,4096]{4,3,2,1,0:T(8,128)(2,1)S(1)}, bf16[1,16,1,32,4096]{4,3,2,1,0:T(8,128)(2,1)}, u32[]{:S(2)}) copy-start(bf16[1,16,1,32,4096]{4,3,2,1,0:T(8,128)(2,1)} %param.10) | copy-start | bytes 12582916
  137.5 4.5 %copy-start = (bf16[4096,256]{1,0:T(8,128)(2,1)S(1)}, bf16[4096,256]{1,0:T(8,128)(2,1)}, u32[]{:S(2)}) copy-start(bf16[4096,256]{1,0:T(8,128)(2,1)} %squeeze_reshape_transpose_reshape.7) | copy-start | bytes 6291460
  196.7 36.0 %all-to-all-start.1 = ((bf16[16,32,1024]{2,1,0:T(8,128)(2,1)}), bf16[16,32,1024]{2,1,0:T(8,128)(2,1)S(1)}, u32[]{:S(2)}, u32[]{:S(2)}) async-start(bf16[16,32,1024]{2,1,0:T(8,128)(2,1)} %bitcast.78), calls=%async_computation.2 | async-start | bytes 2097152 | tf_op jit(solution)/shard_map/all_to_all | solution.py:124
  204.6 51.6 %all-gather.7.cloned.1.call-start = ((), (), s32[]{:S(2)}) async-start(), calls=%async_computation.7 | async-start | bytes 1310720 | tf_op jit(solution)/shard_map/all_gather | solution.py:128
  236.0 91.7 %reduce-scatter.5.cloned.1.call-start = ((), (), s32[]{:S(2)}) async-start(), calls=%async_computation.8 | async-start | bytes 7864320 | tf_op jit(solution)/shard_map/reduce_scatter | solution.py:25
  236.3 3.7 %copy-start.5 = (bf16[1,16,1,32,4096]{4,3,2,1,0:T(8,128)(2,1)S(1)}, bf16[1,16,1,32,4096]{4,3,2,1,0:T(8,128)(2,1)}, u32[]{:S(2)}) copy-start(bf16[1,16,1,32,4096]{4,3,2,1,0:T(8,128)(2,1)} %param.10) | copy-start | bytes 12582916
  330.6 2.6 copy-start.1
Sparse Core Ops, SparseCore 0:
  12.7 71.5 all-gather.8
  86.1 51.3 all-gather.4
  146.9 49.7 reduce-scatter.2
  236.1 20.0 all-gather.6
  258.6 68.9 reduce-scatter.4
where the time goes:
time: 341 us
  waiting for transfers between devices  178 us (52%)
  blocking collectives  60.9 us (18%)
  local copies, waits for them, and re-layouts  46.1 us (14%)
  matrix products  21.6 us (6%)
  between operations  14.1 us (4%)
  other arithmetic  11.1 us (3%)
  starting transfers between devices  8.59 us (3%)
    reduce_scatter x1, waiting for transfers between devices, own_rows(): lax.psum_scatter(whole, axis, scatter_dimension=0, tiled=True)  71.4 us
    all_to_all x1, blocking collectives, on_device(): lax.all_to_all(outgoing.reshape(experts, capacity, narrow), 'ep', split_a...  37.3 us
    all_gather x1, waiting for transfers between devices, gather_together(): lines, at, outs = (lax.all_gather(ravelled, axis), 0, [])  26.2 us
    reduce_scatter x1, waiting for transfers between devices, on_device(): lax.psum_scatter(slot_part.astype(jnp.bfloat16), 'tp', scatter_dimension=...  26.2 us
    all_to_all x1, waiting for transfers between devices, on_device(): lax.all_to_all(leaving[0], 'ep', split_axis=0, concat_axis=0, tiled=True)  25.3 us
    all_gather x1, waiting for transfers between devices, on_device(): lax.all_gather(arrived.reshape(-1, narrow), 'tp', axis=1, tiled=True)  19.4 us
    all_to_all x1, blocking collectives, on_device(): lax.all_to_all(leaving[1], 'ep', split_axis=0, concat_axis=0, tiled=True)  17 us
    unnamed x20, local copies, waits for them, and re-layouts  11.3 us
  transfers between devices with their start and end apart: 6, of which 6 were waited for; matrix products, arithmetic and copies ran while one was open for 16% of the time, Pallas kernels for 0%

commit v1 on v0

v1 whole, which is shorter than its diff:
```python
import functools

import jax
import jax.numpy as jnp
from jax import lax
from jax.experimental import pallas as pl
from jax.experimental.pallas import tpu as pltpu
from jax.sharding import PartitionSpec as P


CHUNKS = 2
RING = 4
LANES = 128
VMEM_LIMIT = 48 << 20


def shift(x, axis, step):
    n = lax.axis_size(axis)
    return lax.ppermute(x, axis, [(i, (i + step) % n) for i in range(n)])


def exchange(x):
    return lax.all_to_all(x, "ep", split_axis=0, concat_axis=0, tiled=True)


def ring_gather(block, axis):
    half = block.shape[0] // 2
    prev = shift(block, axis, 1)
    following = shift(block, axis, -1)
    far_top = shift(prev[:half], axis, 1)
    far_bottom = shift(following[half:], axis, -1)
    return block, following, far_top, far_bottom, prev


def ring_reduce(following, far_top, far_bottom, prev, axis):
    top = shift(far_top, axis, 1)
    bottom = shift(far_bottom, axis, -1)
    following = add_half(following, top, 0)
    prev = add_half(prev, bottom, 1)
    from_prev = shift(following, axis, 1)
    from_next = shift(prev, axis, -1)
    return from_prev, from_next


def call(kernel, out_shape, **options):
    return pl.pallas_call(
        kernel,
        out_shape=out_shape,
        compiler_params=pltpu.CompilerParams(vmem_limit_bytes=VMEM_LIMIT),
        **options,
    )


def bf16(*shape):
    return jax.ShapeDtypeStruct(shape, jnp.bfloat16)


def f32(*shape):
    return jax.ShapeDtypeStruct(shape, jnp.float32)


def dot(left, right, left_dim=1, right_dim=0):
    return lax.dot_general(
        left, right, (((left_dim,), (right_dim,)), ((), ())), preferred_element_type=jnp.float32
    )


def add_half(whole, half, index):
    def kernel(whole_ref, half_ref, out_ref):
        total = whole_ref[...].astype(jnp.float32) + half_ref[...].astype(jnp.float32)
        out_ref[...] = total.astype(jnp.bfloat16)

    spec = pl.BlockSpec(half.shape, lambda i: (index, 0))
    return call(
        kernel,
        bf16(*whole.shape),
        grid=(1,),
        in_specs=[spec, pl.BlockSpec(half.shape, lambda i: (0, 0))],
        out_specs=spec,
        input_output_aliases={0: 0},
    )(whole, half)


def pack(w_gate, w_up, w_down):
    depth, width = w_gate.shape

    def kernel(gate_ref, up_ref, down_ref, out_ref):
        out_ref[:depth] = gate_ref[...]
        out_ref[depth : 2 * depth] = up_ref[...]
        for c in range(depth // width):
            out_ref[pl.ds(2 * depth + c * width, width)] = down_ref[:, c * width : (c + 1) * width]

    return call(kernel, bf16(3 * depth, width))(w_gate, w_up, w_down)


def weight_parts(refs, r, depth):
    half = depth // 2
    if r == 2:
        places = [(refs[2], i * half) for i in range(3)] + [(refs[3], i * half) for i in range(3)]
    else:
        ref = refs[(0, 1, None, 4)[r]]
        places = [(ref, i * half) for i in range(6)]
    return places[0:2], places[2:4], places[4:6]


def activations(here, routed_inputs, weights, width):
    _, sources, _, capacity, model_width = routed_inputs.shape
    depth = model_width // RING
    part = capacity // CHUNKS
    rows = sources * part
    half = depth // 2

    def kernel(here_ref, x_ref, w0, w1, w2, w3, w4, hidden_ref, silu_ref, slope_ref, gate, up):
        refs = (w0, w1, w2, w3, w4)
        step = pl.program_id(0)
        for r in range(RING):

            @pl.when(step == r)
            def _():
                gates, ups, _ = weight_parts(refs, r, depth)
                for h in range(CHUNKS):
                    x = x_ref[0, :, 0, h * part : (h + 1) * part, :].reshape(rows, depth)
                    own = slice(h * rows, (h + 1) * rows)
                    for pieces, total in ((gates, gate), (ups, up)):
                        value = sum(
                            dot(x[:, i * half : (i + 1) * half], ref[pl.ds(first, half)])
                            for i, (ref, first) in enumerate(pieces)
                        )
                        total[own] = value if r == 0 else total[own] + value

        @pl.when(step == RING - 1)
        def _():
            gate_act, up_act = gate[...], up[...]
            sigmoid_gate = jax.nn.sigmoid(gate_act)
            silu_gate = gate_act * sigmoid_gate
            hidden_ref[...] = (silu_gate * up_act).astype(jnp.bfloat16)
            silu_ref[...] = silu_gate
            slope_ref[...] = up_act * sigmoid_gate * (1.0 + gate_act * (1.0 - sigmoid_gate))

    slots = sources * capacity
    whole = pl.BlockSpec(memory_space=pltpu.VMEM)
    return call(
        kernel,
        (bf16(slots, width), f32(slots, width), f32(slots, width)),
        grid_spec=pltpu.PrefetchScalarGridSpec(
            num_scalar_prefetch=1,
            grid=(RING,),
            in_specs=[
                pl.BlockSpec(
                    (1, sources, 1, capacity, depth),
                    lambda i, here: (0, 0, 0, 0, (here[0] + i) % RING),
                )
            ]
            + [whole] * 5,
            out_specs=(pl.BlockSpec((slots, width), lambda i, here: (0, 0)),) * 3,
            scratch_shapes=[pltpu.VMEM((slots, width), jnp.float32)] * 2,
        ),
    )(here, routed_inputs, *weights)


def gradients(here, h, scaled, weights, hidden, silu, slope):
    rows, depth = scaled[0].shape
    width = hidden.shape[1]
    half = depth // 2
    blocks = depth // width

    def kernel(here_ref, *refs):
        scaled_refs, weight_refs, refs = refs[:5], refs[5:10], refs[10:]
        hidden_ref, silu_ref, slope_ref, refs = *refs[:3], refs[3:]
        pair_ref, extra_ref, own_ref, next_ref, top_ref, bottom_ref, prev_ref, by_r, refs = (
            *refs[:8],
            refs[8:],
        )
        parts, sems = refs
        t = here_ref[1]
        copies = []
        for i, (q, first, count) in enumerate(
            (
                (0, 0, rows),
                (1, 0, rows),
                (2, 0, rows // 2),
                (2, rows // 2, rows // 2),
                (3, 0, rows),
            )
        ):
            copies.append(
                pltpu.make_async_copy(
                    scaled_refs[i],
                    by_r.at[(t + q) % RING, pl.ds(first, count)],
                    sems.at[i],
                )
            )
        for copy in copies:
            copy.start()
        for copy in copies:
            copy.wait()
        hidden_grad = jnp.zeros((rows, width), jnp.float32)
        for r in range(RING):
            _, _, downs = weight_parts(weight_refs, r, depth)
            for c in range(blocks):
                ref, first = downs[c * 2 // blocks]
                first += (c % (blocks // 2)) * width
                hidden_grad += dot(
                    by_r[r, :, c * width : (c + 1) * width], ref[pl.ds(first, width)], 1, 1
                )
        products = jnp.sum(
            hidden_grad * hidden_ref[...].astype(jnp.float32), axis=1, keepdims=True
        )
        high = products.astype(jnp.bfloat16).astype(jnp.float32)
        lane = lax.broadcasted_iota(jnp.int32, (rows, LANES), 1)
        extra = jnp.where(lane == 0, high, jnp.where(lane == 1, products - high, 0.0))
        extra_ref[...] = extra.astype(jnp.bfloat16)
        gate_grad = (hidden_grad * slope_ref[...]).astype(jnp.bfloat16)
        up_grad = (hidden_grad * silu_ref[...]).astype(jnp.bfloat16)
        pair_ref[:, :width] = gate_grad
        pair_ref[:, width:] = up_grad
        for r in range(RING):
            gates, ups, _ = weight_parts(weight_refs, r, depth)
            q = (r - t + RING) % RING
            for i in range(2):
                gate_ref, gate_first = gates[i]
                up_ref, up_first = ups[i]
                value = dot(gate_grad, gate_ref[pl.ds(gate_first, half)], 1, 1)
                value += dot(up_grad, up_ref[pl.ds(up_first, half)], 1, 1)
                parts[q, :, i * half : (i + 1) * half] = value.astype(jnp.bfloat16)
        own_ref[...] = parts[0]
        next_ref[...] = parts[1]
        top_ref[...] = parts[2, : rows // 2]
        bottom_ref[...] = parts[2, rows // 2 :]
        prev_ref[...] = parts[3]

    anywhere = pl.BlockSpec(memory_space=pl.ANY)
    whole = pl.BlockSpec(memory_space=pltpu.VMEM)
    mine = pl.BlockSpec((rows, width), lambda i, here: (h, 0))
    return call(
        kernel,
        (
            bf16(rows, 2 * width),
            bf16(rows, LANES),
            bf16(rows, depth),
            bf16(rows, depth),
            bf16(rows // 2, depth),
            bf16(rows // 2, depth),
            bf16(rows, depth),
            bf16(RING, rows, depth),
        ),
        grid_spec=pltpu.PrefetchScalarGridSpec(
            num_scalar_prefetch=1,
            grid=(1,),
            in_specs=[anywhere] * 5 + [whole] * 5 + [mine] * 3,
            out_specs=(whole,) * 8,
            scratch_shapes=[
                pltpu.VMEM((RING, rows, depth), jnp.bfloat16),
                pltpu.SemaphoreType.DMA((5,)),
            ],
        ),
    )(here, *scaled, *weights, hidden, silu, slope)


def weight_chunk(here, r, routed_inputs, hidden, pairs, scaled, received=None):
    _, sources, _, capacity, model_width = routed_inputs.shape
    depth = model_width // RING
    part = capacity // CHUNKS
    rows = sources * part
    width = hidden.shape[1]
    half = depth // 2

    def kernel(here_ref, x_ref, hidden_ref, *refs):
        pair_refs, scaled_refs, refs = refs[:CHUNKS], refs[CHUNKS : 2 * CHUNKS], refs[2 * CHUNKS :]

        def inputs(h, i):
            x = x_ref[0, :, 0, h * part : (h + 1) * part, i * half : (i + 1) * half]
            return x.reshape(rows, half)

        for i in range(6):
            if i < 4:
                lanes = slice((i // 2) * width, (i // 2 + 1) * width)
                value = sum(
                    dot(inputs(h, i % 2), pair_refs[h][:, lanes], 0, 0) for h in range(CHUNKS)
                )
                values = [(value, slice(0, half))]
            else:
                values = []
                for c in range(half // width):
                    first = (i - 4) * half + c * width
                    value = sum(
                        dot(
                            hidden_ref[h * rows : (h + 1) * rows],
                            scaled_refs[h][0, :, first : first + width],
                            0,
                            0,
                        )
                        for h in range(CHUNKS)
                    )
                    values.append((value, slice(c * width, (c + 1) * width)))
            for value, place in values:
                source = pl.ds(i * half + place.start, place.stop - place.start)
                if r:
                    out_ref = refs[i // 3] if r == 2 else refs[0]
                    at = (i % 3 if r == 2 else i) * half + place.start
                    out_ref[pl.ds(at, place.stop - place.start)] = value.astype(jnp.bfloat16)
                    continue
                value += refs[0][source].astype(jnp.float32) + refs[1][source].astype(jnp.float32)
                if i < 4:
                    refs[2 + i // 2][pl.ds((i % 2) * half, half)] = value
                else:
                    first = (i - 4) * half + place.start
                    refs[4][:, first : first + width] = value

    whole = pl.BlockSpec(memory_space=pltpu.VMEM)
    chunk = pl.BlockSpec((1, rows, depth), lambda i, here: (r, 0, 0))
    if r == 0:
        outs = (f32(depth, width), f32(depth, width), f32(width, depth))
    elif r == 2:
        outs = (bf16(3 * half, width), bf16(3 * half, width))
    else:
        outs = (bf16(6 * half, width),)
    received = received or ()
    return call(
        kernel,
        outs,
        grid_spec=pltpu.PrefetchScalarGridSpec(
            num_scalar_prefetch=1,
            grid=(1,),
            in_specs=[
                pl.BlockSpec(
                    (1, sources, 1, capacity, depth),
                    lambda i, here: (0, 0, 0, 0, (here[0] + r) % RING),
                ),
                whole,
            ]
            + [whole] * CHUNKS
            + [chunk] * CHUNKS
            + [whole] * len(received),
            out_specs=(whole,) * len(outs),
        ),
    )(here, routed_inputs, hidden, *pairs, *scaled, *received)


def leaving_rows(own, from_prev, from_next, extra):
    rows, narrow = own.shape

    def kernel(own_ref, prev_ref, next_ref, extra_ref, out_ref):
        total = own_ref[...].astype(jnp.float32) + prev_ref[...].astype(jnp.float32)
        total += next_ref[...].astype(jnp.float32)
        out_ref[:, :narrow] = total.astype(jnp.bfloat16)
        out_ref[:, narrow:] = extra_ref[...]

    return call(kernel, bf16(rows, narrow + LANES))(own, from_prev, from_next, extra)


def token_rows(slot_index, back):
    tokens = slot_index.shape[0]
    rows, wide = back[0].shape
    narrow = wide - LANES

    def kernel(slot_ref, *refs):
        back_refs, out_ref = refs[:CHUNKS], refs[CHUNKS]
        total = jnp.zeros((tokens, narrow), jnp.float32)
        chosen = [jnp.zeros((tokens, LANES), jnp.float32)] * 2
        for h in range(CHUNKS):
            slot = lax.broadcasted_iota(jnp.int32, (tokens, rows), 1) + h * rows
            picks = [
                jnp.where(slot_ref[:, k : k + 1] == slot, 1.0, 0.0).astype(jnp.bfloat16)
                for k in range(2)
            ]
            total += dot(picks[0] + picks[1], back_refs[h][:, :narrow])
            chosen = [c + dot(p, back_refs[h][:, narrow:]) for c, p in zip(chosen, picks)]
        out_ref[:, :narrow] = total.astype(jnp.bfloat16)
        lane = lax.broadcasted_iota(jnp.int32, (tokens, LANES), 1)
        tail = jnp.zeros((tokens, LANES), jnp.float32)
        for k in range(2):
            value = chosen[k][:, 0:1] + chosen[k][:, 1:2]
            high = value.astype(jnp.bfloat16).astype(jnp.float32)
            tail = jnp.where(lane == 2 * k, high, jnp.where(lane == 2 * k + 1, value - high, tail))
        out_ref[:, narrow:] = tail.astype(jnp.bfloat16)

    return call(kernel, bf16(tokens, wide))(slot_index, *back)


def finish_tokens(here, gate_probs, gathered):
    tokens, wide = gathered[0].shape
    narrow = wide - LANES

    def kernel(here_ref, probs_ref, *refs):
        out_ref, logit_ref = refs[RING:]
        total = jnp.zeros((tokens, LANES), jnp.float32)
        for q in range(RING):
            first = ((here_ref[0] + here_ref[1] + q) % RING) * narrow
            out_ref[:, pl.ds(pl.multiple_of(first, LANES), narrow)] = refs[q][:, :narrow]
            total += refs[q][:, narrow:].astype(jnp.float32)
        chosen = [
            (total[:, 2 * k : 2 * k + 1] + total[:, 2 * k + 1 : 2 * k + 2])
            .astype(jnp.bfloat16)
            .astype(jnp.float32)
            for k in range(2)
        ]
        both = chosen[0] + chosen[1]
        for k in range(2):
            logit_ref[:, k : k + 1] = chosen[k] - probs_ref[:, k : k + 1] * both

    whole = pl.BlockSpec(memory_space=pltpu.VMEM)
    return call(
        kernel,
        (bf16(tokens, RING * narrow), f32(tokens, 2)),
        grid_spec=pltpu.PrefetchScalarGridSpec(
            num_scalar_prefetch=1,
            grid=(1,),
            in_specs=[whole] * (RING + 1),
            out_specs=(whole,) * 2,
        ),
    )(here, gate_probs, *gathered)


def slots_of(routes, experts, capacity):
    tokens = routes.shape[0]
    part = capacity // CHUNKS
    hot = (routes[:, :, None] == jnp.arange(experts, dtype=jnp.int32)).astype(jnp.bfloat16)
    before = jnp.arange(tokens)[:, None] > jnp.arange(tokens)[None, :]
    earlier = dot(before.astype(jnp.bfloat16), hot[:, 0] + hot[:, 1])
    place = jnp.sum(earlier[:, None, :] * hot.astype(jnp.float32), axis=2).astype(jnp.int32)
    return (place // part) * (experts * part) + routes * part + place % part


def layer(out_grad, routes, chosen_logits, routed_inputs, w_gate, w_up, w_down):
    experts = lax.axis_size("ep")
    f, t = lax.axis_index("fsdp"), lax.axis_index("tp")
    here = jnp.stack([f, t]).astype(jnp.int32)
    model_width = out_grad.shape[1]
    capacity = routed_inputs.shape[3]
    part = capacity // CHUNKS
    rows = experts * part
    slots = experts * capacity
    narrow = model_width // RING
    width = w_gate.shape[2]

    weights = ring_gather(pack(w_gate[0], w_up[0], w_down[0]), "fsdp")

    gate_probs = jax.nn.softmax(chosen_logits, axis=-1)
    slot_index = slots_of(routes, experts, capacity)
    picks = (slot_index[:, :, None] == jnp.arange(slots, dtype=jnp.int32)).astype(jnp.bfloat16)
    mine = (f + t) % RING
    piece = lax.dynamic_slice_in_dim(out_grad, mine * narrow, narrow, 1).astype(jnp.float32)
    weighted = (gate_probs[:, :, None] * piece[:, None, :]).astype(jnp.bfloat16)
    outgoing = lax.dot_general(
        picks, weighted, (((0, 1), (0, 1)), ((), ())), preferred_element_type=jnp.float32
    ).astype(jnp.bfloat16)
    outgoing = outgoing.reshape(CHUNKS, experts, part, narrow)
    arrived = [
        ring_gather(exchange(outgoing[h]).reshape(rows, narrow), "tp")
        for h in range(CHUNKS)
    ]

    hidden, silu, slope = activations(here, routed_inputs, weights, width)
    pairs, scaled, back = [], [], []
    for h in range(CHUNKS):
        pair, extra, own, following, top, bottom, prev, by_r = gradients(
            here, h, arrived[h], weights, hidden, silu, slope
        )
        pairs.append(pair)
        scaled.append(by_r)
        received = ring_reduce(following, top, bottom, prev, "tp")
        leaving = leaving_rows(own, *received, extra)
        leaving = leaving.reshape(experts, part, narrow + LANES)
        back.append(exchange(leaving).reshape(rows, narrow + LANES))

    chunk = functools.partial(
        weight_chunk, here, routed_inputs=routed_inputs, hidden=hidden, pairs=pairs, scaled=scaled
    )
    received = ring_reduce(*chunk(1), *chunk(2), *chunk(3), "fsdp")
    grad_gate, grad_up, grad_down = chunk(0, received=received)

    mine_rows = token_rows(slot_index, back)
    gathered = [mine_rows] + [shift(mine_rows, "tp", -q) for q in range(1, RING)]
    input_grad, logit_grad = finish_tokens(here, gate_probs, gathered)
    return input_grad, logit_grad, grad_gate[None], grad_up[None], grad_down[None]


def solution(mesh):
    return jax.shard_map(
        layer,
        mesh=mesh,
        in_specs=(
            P(("ep", "fsdp"), None),
            P(("ep", "fsdp"), None),
            P(("ep", "fsdp"), None),
            P("ep", None, "fsdp", None, None),
            P("ep", "fsdp", "tp"),
            P("ep", "fsdp", "tp"),
            P("ep", "tp", "fsdp"),
        ),
        out_specs=(
            P(("ep", "fsdp"), None),
            P(("ep", "fsdp"), None),
            P("ep", "fsdp", "tp"),
            P("ep", "fsdp", "tp"),
            P("ep", "tp", "fsdp"),
        ),
        check_vma=False,
    )
```

time: 341 us -> 223 us (0.65)
  waiting for transfers between devices: 178 us -> 68.2 us
  starting transfers between devices: 8.59 us -> 62.1 us
  Pallas kernels: 0 us -> 48.8 us
  blocking collectives: 60.9 us -> 26.5 us
  local copies, waits for them, and re-layouts: 46.1 us -> 11.8 us
  matrix products: 21.6 us -> 1.72 us
  between operations: 14.1 us -> 0.99 us
  other arithmetic: 11.1 us -> 2.07 us
    reduce_scatter x2 -> x0, waiting for transfers between devices: 97.6 us -> none  [the longest x1 71.4 us: own_rows(): lax.psum_scatter(whole, axis, scatter_dimension=0, tiled=True)]
    all_gather x3 -> x0, waiting for transfers between devices: 55.4 us -> none  [the longest x1 26.2 us: gather_together(): lines, at, outs = (lax.all_gather(ravelled, axis), 0, [])]
    ppermute x0 -> x27, waiting for transfers between devices: none -> 49.7 us  [shift(): return lax.ppermute(x, axis, [(i, (i + step) % n) for i in range(n)])]
    pallas_call x0 -> x18, Pallas kernels: none -> 48.8 us  [the longest x4 16.5 us: weight_chunk(): call(kernel, outs, grid_spec=pltpu.PrefetchScalarGridSpec(num_scalar_pref...]
    ppermute x0 -> x27, starting transfers between devices: none -> 35.9 us  [shift(): return lax.ppermute(x, axis, [(i, (i + step) % n) for i in range(n)])]
    all_to_all x2 -> x1, blocking collectives: 54.2 us -> 26.5 us  [exchange(): return lax.all_to_all(x, 'ep', split_axis=0, concat_axis=0, tiled=True)]
    dot_general x7 -> x2, matrix products: 21.6 us -> 1.72 us  [the longest x1 1.59 us: layer(): lax.dot_general(picks, weighted, (((0, 1), (0, 1)), ((), ())), preferred_...]
    all_to_all x1 -> x3, starting transfers between devices: 7.94 us -> 26.2 us  [exchange(): return lax.all_to_all(x, 'ep', split_axis=0, concat_axis=0, tiled=True)]
  transfers between devices with their start and end apart: 6 -> 30, of which waited for: 6 -> 11; matrix products, arithmetic and copies ran while one was open for 16% -> 4% of each run, Pallas kernels for 0% -> 20%
where the time goes in v1:
time: 223 us; the launch traced here: 222 us
  waiting for transfers between devices  68.2 us (31%)
  starting transfers between devices  62.1 us (28%)
  Pallas kernels  48.8 us (22%)
  blocking collectives  26.5 us (12%)
  local copies, waits for them, and re-layouts  11.8 us (5%)
    ppermute x27, waiting for transfers between devices, shift(): return lax.ppermute(x, axis, [(i, (i + step) % n) for i in range(n)])  49.7 us
    ppermute x27, starting transfers between devices, shift(): return lax.ppermute(x, axis, [(i, (i + step) % n) for i in range(n)])  35.9 us
    all_to_all x1, blocking collectives, exchange(): return lax.all_to_all(x, 'ep', split_axis=0, concat_axis=0, tiled=True)  26.5 us
    all_to_all x3, starting transfers between devices, exchange(): return lax.all_to_all(x, 'ep', split_axis=0, concat_axis=0, tiled=True)  26.2 us
    all_to_all x3, waiting for transfers between devices, exchange(): return lax.all_to_all(x, 'ep', split_axis=0, concat_axis=0, tiled=True)  18.5 us
    pallas_call x4, Pallas kernels, weight_chunk(): call(kernel, outs, grid_spec=pltpu.PrefetchScalarGridSpec(num_scalar_pref...  16.5 us
    pallas_call x2, Pallas kernels, gradients(): call(kernel, (bf16(rows, 2 * width), bf16(rows, LANES), bf16(rows, depth)...  16.1 us
    unnamed x41, local copies, waits for them, and re-layouts  7.87 us
  transfers between devices with their start and end apart: 30, of which 11 were waited for; matrix products, arithmetic and copies ran while one was open for 4% of the time, Pallas kernels for 20%

profile of v1, /device:TPU:1, one launch (start us, length us, event | category | flops | bytes accessed | tf_op | source)
XLA Modules:
  0.0 222.2 jit_solution(2984600709286423987)
XLA Ops:
  3.9 3.4 %collective-permute-start.4 = (bf16[3072,256]{1,0:T(8,128)(2,1)S(1)}, bf16[3072,256]{1,0:T(8,128)(2,1)S(1)}, u32[]{:S(2)}, u32[]{:S(2)}) collective-permute-start(bf16[3072,256]{1,0:T(8,128)(2,1)S(1)} %shard_map.110.w0.refs_5_), channel_id=1, source_target_pairs={{0,12},{4,0},{8,4},{12,8},{1,13},{5,1},{9,5},{13,9},{2,14},{6,2},{... | collective-permute-start | bytes 4718600 | tf_op jit(solution)/shard_map/ppermute | solution.py:19
  12.1 26.5 %all_to_all.20 = bf16[16,16,1024]{2,1,0:T(8,128)(2,1)} all-to-all(bf16[16,16,1024]{2,1,0:T(8,128)(2,1)S(1)} %bitcast.29), channel_id=1, replica_groups=mesh['ep'=16,'fsdp'=4,'tp'=4] {'ep'}, dimensions={0} | all-to-all | bytes 1048576 | tf_op jit(solution)/shard_map/all_to_all | solution.py:23
  38.6 4.1 %all-to-all-start.2 = ((bf16[16,16,1024]{2,1,0:T(8,128)(2,1)}), bf16[16,16,1024]{2,1,0:T(8,128)(2,1)}, u32[]{:S(2)}, u32[]{:S(2)}) async-start(bf16[16,16,1024]{2,1,0:T(8,128)(2,1)} %bitcast.28), calls=%async_computation.2 | async-start | bytes 1048576 | tf_op jit(solution)/shard_map/all_to_all | solution.py:23
  45.9 2.6 %collective-permute-start.7 = (bf16[1536,256]{1,0:T(8,128)(2,1)S(1)}, bf16[1536,256]{1,0:T(8,128)(2,1)S(1)}, u32[]{:S(2)}, u32[]{:S(2)}) collective-permute-start(bf16[1536,256]{1,0:T(8,128)(2,1)S(1)} %slice.48), channel_id=1, source_target_pairs={{0,12},{4,0},{8,4},{12,8},{1,13},{5,1},{9,5},{13,9},{2,14},{6,2},{... | collective-permute-start | bytes 2359304 | tf_op jit(solution)/shard_map/ppermute | solution.py:19
  50.4 7.3 %collective-permute-done.1.refs_4_ = bf16[256,1024]{1,0:T(8,128)(2,1)S(1)} collective-permute-done((bf16[256,1024]{1,0:T(8,128)(2,1)}, bf16[256,1024]{1,0:T(8,128)(2,1)S(1)}, u32[]{:S(2)}, u32[]{:S(2)}) %collective-permute-start.1) | collective-permute-done | bytes 524320 | tf_op jit(solution)/shard_map/ppermute | solution.py:19
  65.0 5.9 %shard_map.111 = (bf16[512,256]{1,0:T(8,128)(2,1)S(1)}, f32[512,256]{1,0:T(8,128)S(1)}, f32[512,256]{1,0:T(8,128)S(1)}) custom-call(s32[2]{0:T(128)S(1)} %pad_add_fusion.here_ref, bf16[1,16,1,32,4096]{4,3,2,1,0:T(8,128)(2,1)} %x_ref.9, bf16[3072,256]{1,0:T(8,128)(2,1)S(1)} %shard_map.110.w0.refs_5_, bf16[3072,256]{1,0:T(8,128)(2,1)S(1)} %collective-permute-done.4.w1.refs_6_, ...), custom_call_target="tpu_custom_call" | custom-call | tf_op jit(solution)/shard_map/pallas_call | solution.py:142
  71.1 7.4 %shard_map.112 = (bf16[256,512]{1,0:T(8,128)(2,1)S(1)}, bf16[256,128]{1,0:T(8,128)(2,1)S(1)}, bf16[256,1024]{1,0:T(8,128)(2,1)S(1)}, bf16[256,1024]{1,0:T(8,128)...) custom-call(s32[2]{0:T(128)S(1)} %pad_add_fusion.here_ref, ...), custom_call_target="tpu_custom_call" | custom-call | tf_op jit(solution)/shard_map/pallas_call | solution.py:235
  86.6 2.7 %collective-permute-start.11 = (bf16[256,1024]{1,0:T(8,128)(2,1)S(1)}, bf16[256,1024]{1,0:T(8,128)(2,1)S(1)}, u32[]{:S(2)}, u32[]{:S(2)}) collective-permute-start(bf16[256,1024]{1,0:T(8,128)(2,1)S(1)} %shard_map.114), channel_id=1, source_target_pairs={{0,3},{1,0},{2,1},{3,2},{4,7},{5,4},{6,5},{7,6},{8,11},{9,8},{10,9... | collective-permute-start | bytes 1572872 | tf_op jit(solution)/shard_map/ppermute | solution.py:19
  89.3 8.0 %collective-permute-done.13.refs_4_ = bf16[256,1024]{1,0:T(8,128)(2,1)S(1)} collective-permute-done((bf16[256,1024]{1,0:T(8,128)(2,1)}, bf16[256,1024]{1,0:T(8,128)(2,1)S(1)}, u32[]{:S(2)}, u32[]{:S(2)}) %collective-permute-start.13) | collective-permute-done | bytes 524320 | tf_op jit(solution)/shard_map/ppermute | solution.py:19
  101.5 7.0 %collective-permute-done.9.prev_ref = bf16[256,1024]{1,0:T(8,128)(2,1)S(1)} collective-permute-done((bf16[256,1024]{1,0:T(8,128)(2,1)S(1)}, bf16[256,1024]{1,0:T(8,128)(2,1)S(1)}, u32[]{:S(2)}, u32[]{:S(2)}) %collective-permute-start.9) | collective-permute-done | bytes 524320 | tf_op jit(solution)/shard_map/ppermute | solution.py:19
  109.5 12.6 %all-to-all-start.1 = ((bf16[16,16,1152]{2,1,0:T(8,128)(2,1)}), bf16[16,16,1152]{2,1,0:T(8,128)(2,1)}, u32[]{:S(2)}, u32[]{:S(2)}) async-start(bf16[16,16,1152]{2,1,0:T(8,128)(2,1)} %bitcast.9), calls=%async_computation.1 | async-start | bytes 1179648 | tf_op jit(solution)/shard_map/all_to_all | solution.py:23
  125.4 8.7 %shard_map.116 = (bf16[256,512]{1,0:T(8,128)(2,1)S(1)}, bf16[256,128]{1,0:T(8,128)(2,1)S(1)}, bf16[256,1024]{1,0:T(8,128)(2,1)S(1)}, bf16[256,1024]{1,0:T(8,128)...) custom-call(s32[2]{0:T(128)S(1)} %pad_add_fusion.here_ref, ...), custom_call_target="tpu_custom_call" | custom-call | tf_op jit(solution)/shard_map/pallas_call | solution.py:235
  134.1 3.0 %shard_map.123 = (bf16[1536,256]{1,0:T(8,128)(2,1)S(1)}, bf16[1536,256]{1,0:T(8,128)(2,1)S(1)}) custom-call(s32[2]{0:T(128)S(1)} %pad_add_fusion.here_ref, bf16[1,16,1,32,4096]{4,3,2,1,0:T(8,128)(2,1)} %x_ref.9, bf16[512,256]{1,0:T(8,128)(2,1)S(1)} %get-tuple-element.31.refs_10_.hidden_ref, bf16[256,512]{1,0:T(8,128)(2,1)S(1)} %get-tuple-element.48.refs_0_, ...), custom_call_target="tpu_custom_call" | custom-call | tf_op jit(solution)/shard_map/pallas_call | solution.py:319
  137.2 2.7 %collective-permute-start.25 = (bf16[1536,256]{1,0:T(8,128)(2,1)S(1)}, bf16[1536,256]{1,0:T(8,128)(2,1)S(1)}, u32[]{:S(2)}, u32[]{:S(2)}) collective-permute-start(bf16[1536,256]{1,0:T(8,128)(2,1)S(1)} %get-tuple-element.53), channel_id=1, source_target_pairs={{0,12},{4,0},{8,4},{12,8},{1,13},{5,1},{9,5},{13,9},{2,14},{6,2},{... | collective-permute-start | bytes 2359304 | tf_op jit(solution)/shard_map/ppermute | solution.py:19
  142.6 5.8 %collective-permute-done.16.half_ref = bf16[128,1024]{1,0:T(8,128)(2,1)S(1)} collective-permute-done((bf16[128,1024]{1,0:T(8,128)(2,1)S(1)}, bf16[128,1024]{1,0:T(8,128)(2,1)S(1)}, u32[]{:S(2)}, u32[]{:S(2)}) %collective-permute-start.16) | collective-permute-done | bytes 262176 | tf_op jit(solution)/shard_map/ppermute | solution.py:19
  148.8 2.7 %collective-permute-start.19 = (bf16[256,1024]{1,0:T(8,128)(2,1)S(1)}, bf16[256,1024]{1,0:T(8,128)(2,1)S(1)}, u32[]{:S(2)}, u32[]{:S(2)}) collective-permute-start(bf16[256,1024]{1,0:T(8,128)(2,1)S(1)} %shard_map.118), channel_id=1, source_target_pairs={{0,3},{1,0},{2,1},{3,2},{4,7},{5,4},{6,5},{7,6},{8,11},{9,8},{10,9... | collective-permute-start | bytes 1572872 | tf_op jit(solution)/shard_map/ppermute | solution.py:19
  151.6 4.2 %shard_map.122.whole_ref = bf16[3072,256]{1,0:T(8,128)(2,1)} custom-call(s32[2]{0:T(128)S(1)} %pad_add_fusion.here_ref, bf16[1,16,1,32,4096]{4,3,2,1,0:T(8,128)(2,1)} %x_ref.9, bf16[512,256]{1,0:T(8,128)(2,1)S(1)} %get-tuple-element.31.refs_10_.hidden_ref, bf16[256,512]{1,0:T(8,128)(2,1)S(1)} %get-tuple-element.48.refs_0_, ...), custom_call_target="tpu_custom_call" | custom-call | tf_op jit(solution)/shard_map/pallas_call | solution.py:319
  155.8 4.2 %shard_map.125.whole_ref = bf16[3072,256]{1,0:T(8,128)(2,1)} custom-call(s32[2]{0:T(128)S(1)} %pad_add_fusion.here_ref, bf16[1,16,1,32,4096]{4,3,2,1,0:T(8,128)(2,1)} %x_ref.9, bf16[512,256]{1,0:T(8,128)(2,1)S(1)} %get-tuple-element.31.refs_10_.hidden_ref, bf16[256,512]{1,0:T(8,128)(2,1)S(1)} %get-tuple-element.48.refs_0_, ...), custom_call_target="tpu_custom_call" | custom-call | tf_op jit(solution)/shard_map/pallas_call | solution.py:319
  164.4 2.7 %collective-permute-start.26 = (bf16[3072,256]{1,0:T(8,128)(2,1)}, bf16[3072,256]{1,0:T(8,128)(2,1)}, u32[]{:S(2)}, u32[]{:S(2)}) collective-permute-start(bf16[3072,256]{1,0:T(8,128)(2,1)} %shard_map.126), channel_id=1, source_target_pairs={{0,12},{4,0},{8,4},{12,8},{1,13},{5,1},{9,5},{13,9},{2,14},{6,2},{... | collective-permute-start | bytes 4718600 | tf_op jit(solution)/shard_map/ppermute | solution.py:19
  168.1 9.5 %all-to-all-start.3 = ((bf16[16,16,1152]{2,1,0:T(8,128)(2,1)}), bf16[16,16,1152]{2,1,0:T(8,128)(2,1)}, u32[]{:S(2)}, u32[]{:S(2)}) async-start(bf16[16,16,1152]{2,1,0:T(8,128)(2,1)} %bitcast.21), calls=%async_computation.3 | async-start | bytes 1179648 | tf_op jit(solution)/shard_map/all_to_all | solution.py:23
  177.7 18.5 %all-to-all-done.3 = bf16[16,16,1152]{2,1,0:T(8,128)(2,1)} async-done(((bf16[16,16,1152]{2,1,0:T(8,128)(2,1)}), bf16[16,16,1152]{2,1,0:T(8,128)(2,1)}, u32[]{:S(2)}, u32[]{:S(2)}) %all-to-all-start.3) | async-done | bytes 589856 | tf_op jit(solution)/shard_map/all_to_all | solution.py:23
  199.6 7.6 %collective-permute-done.20.refs_1_ = bf16[128,1152]{1,0:T(8,128)(2,1)S(1)} collective-permute-done((bf16[128,1152]{1,0:T(8,128)(2,1)S(1)}, bf16[128,1152]{1,0:T(8,128)(2,1)S(1)}, u32[]{:S(2)}, u32[]{:S(2)}) %collective-permute-start.20) | collective-permute-done | bytes 294944 | tf_op jit(solution)/shard_map/ppermute | solution.py:19
  208.7 5.9 %collective-permute-done.22.refs_3_ = bf16[128,1152]{1,0:T(8,128)(2,1)S(1)} collective-permute-done((bf16[128,1152]{1,0:T(8,128)(2,1)S(1)}, bf16[128,1152]{1,0:T(8,128)(2,1)S(1)}, u32[]{:S(2)}, u32[]{:S(2)}) %collective-permute-start.22) | collective-permute-done | bytes 294944 | tf_op jit(solution)/shard_map/ppermute | solution.py:19
  217.1 5.1 %shard_map.127 = (f32[1024,256]{1,0:T(8,128)}, f32[1024,256]{1,0:T(8,128)}, f32[256,1024]{1,0:T(8,128)}) custom-call(s32[2]{0:T(128)S(1)} %pad_add_fusion.here_ref, bf16[1,16,1,32,4096]{4,3,2,1,0:T(8,128)(2,1)} %x_ref.9, bf16[512,256]{1,0:T(8,128)(2,1)S(1)} %get-tuple-element.31.refs_10_.hidden_ref, bf16[256,512]{1,0:T(8,128)(2,1)S(1)} %get-tuple-element.48.refs_0_, ...), custom_call_target="tpu_custom_call" | custom-call | tf_op jit(solution)/shard_map/pallas_call | solution.py:319
  (116 shorter events, 53.3 us)
Async XLA Ops:
  3.9 42.0 %collective-permute-start.4 = (bf16[3072,256]{1,0:T(8,128)(2,1)S(1)}, bf16[3072,256]{1,0:T(8,128)(2,1)S(1)}, u32[]{:S(2)}, u32[]{:S(2)}) collective-permute-start(bf16[3072,256]{1,0:T(8,128)(2,1)S(1)} %shard_map.110.w0.refs_5_), channel_id=1, source_target_pairs={{0,12},{4,0},{8,4},{12,8},{1,13},{5,1},{9,5},{13,9},{2,14},{6,2},{... | collective-permute-start | bytes 4718600 | tf_op jit(solution)/shard_map/ppermute | solution.py:19
  7.3 36.9 %collective-permute-start.5 = (bf16[3072,256]{1,0:T(8,128)(2,1)S(1)}, bf16[3072,256]{1,0:T(8,128)(2,1)}, u32[]{:S(2)}, u32[]{:S(2)}) collective-permute-start(bf16[3072,256]{1,0:T(8,128)(2,1)S(1)} %shard_map.110.w0.refs_5_), channel_id=1, source_target_pairs={{0,4},{4,8},{8,12},{12,0},{1,5},{5,9},{9,13},{13,1},{2,6},{6,10},{... | collective-permute-start | bytes 4718600 | tf_op jit(solution)/shard_map/ppermute | solution.py:19
  38.6 42.9 %all-to-all-start.2 = ((bf16[16,16,1024]{2,1,0:T(8,128)(2,1)}), bf16[16,16,1024]{2,1,0:T(8,128)(2,1)}, u32[]{:S(2)}, u32[]{:S(2)}) async-start(bf16[16,16,1024]{2,1,0:T(8,128)(2,1)} %bitcast.28), calls=%async_computation.2 | async-start | bytes 1048576 | tf_op jit(solution)/shard_map/all_to_all | solution.py:23
  42.8 14.9 %collective-permute-start.1 = (bf16[256,1024]{1,0:T(8,128)(2,1)}, bf16[256,1024]{1,0:T(8,128)(2,1)S(1)}, u32[]{:S(2)}, u32[]{:S(2)}) collective-permute-start(bf16[256,1024]{1,0:T(8,128)(2,1)} %bitcast.22), channel_id=1, source_target_pairs={{0,1},{1,2},{2,3},{3,0},{4,5},{5,6},{6,7},{7,4},{8,9},{9,10},{10,1... | collective-permute-start | bytes 1572872 | tf_op jit(solution)/shard_map/ppermute | solution.py:19
  45.3 19.7 %collective-permute-start.6 = (bf16[1536,256]{1,0:T(8,128)(2,1)S(1)}, bf16[1536,256]{1,0:T(8,128)(2,1)S(1)}, u32[]{:S(2)}, u32[]{:S(2)}) collective-permute-start(bf16[1536,256]{1,0:T(8,128)(2,1)S(1)} %slice.47), channel_id=1, source_target_pairs={{0,4},{4,8},{8,12},{12,0},{1,5},{5,9},{9,13},{13,1},{2,6},{6,10},{... | collective-permute-start | bytes 2359304 | tf_op jit(solution)/shard_map/ppermute | solution.py:19
  45.9 19.1 %collective-permute-start.7 = (bf16[1536,256]{1,0:T(8,128)(2,1)S(1)}, bf16[1536,256]{1,0:T(8,128)(2,1)S(1)}, u32[]{:S(2)}, u32[]{:S(2)}) collective-permute-start(bf16[1536,256]{1,0:T(8,128)(2,1)S(1)} %slice.48), channel_id=1, source_target_pairs={{0,12},{4,0},{8,4},{12,8},{1,13},{5,1},{9,5},{13,9},{2,14},{6,2},{... | collective-permute-start | bytes 2359304 | tf_op jit(solution)/shard_map/ppermute | solution.py:19
  48.5 12.0 %collective-permute-start = (bf16[256,1024]{1,0:T(8,128)(2,1)S(1)}, bf16[256,1024]{1,0:T(8,128)(2,1)S(1)}, u32[]{:S(2)}, u32[]{:S(2)}) collective-permute-start(bf16[256,1024]{1,0:T(8,128)(2,1)S(1)} %bitcast.23), channel_id=1, source_target_pairs={{0,3},{1,0},{2,1},{3,2},{4,7},{5,4},{6,5},{7,6},{8,11},{9,8},{10,9... | collective-permute-start | bytes 1572872 | tf_op jit(solution)/shard_map/ppermute | solution.py:19
  57.7 13.4 %collective-permute-start.2 = (bf16[128,1024]{1,0:T(8,128)(2,1)S(1)}, bf16[128,1024]{1,0:T(8,128)(2,1)S(1)}, u32[]{:S(2)}, u32[]{:S(2)}) collective-permute-start(bf16[128,1024]{1,0:T(8,128)(2,1)S(1)} %slice.45), channel_id=1, source_target_pairs={{0,1},{1,2},{2,3},{3,0},{4,5},{5,6},{6,7},{7,4},{8,9},{9,10},{10,1... | collective-permute-start | bytes 786440 | tf_op jit(solution)/shard_map/ppermute | solution.py:19
  60.5 10.5 %collective-permute-start.3 = (bf16[128,1024]{1,0:T(8,128)(2,1)S(1)}, bf16[128,1024]{1,0:T(8,128)(2,1)S(1)}, u32[]{:S(2)}, u32[]{:S(2)}) collective-permute-start(bf16[128,1024]{1,0:T(8,128)(2,1)S(1)} %slice.46), channel_id=1, source_target_pairs={{0,3},{1,0},{2,1},{3,2},{4,7},{5,4},{6,5},{7,6},{8,11},{9,8},{10,9... | collective-permute-start | bytes 786440 | tf_op jit(solution)/shard_map/ppermute | solution.py:19
  81.4 15.8 %collective-permute-start.13 = (bf16[256,1024]{1,0:T(8,128)(2,1)}, bf16[256,1024]{1,0:T(8,128)(2,1)S(1)}, u32[]{:S(2)}, u32[]{:S(2)}) collective-permute-start(bf16[256,1024]{1,0:T(8,128)(2,1)} %bitcast.12.refs_0_), channel_id=1, source_target_pairs={{0,1},{1,2},{2,3},{3,0},{4,5},{5,6},{6,7},{7,4},{8,9},{9,10},{10,1... | collective-permute-start | bytes 1572872 | tf_op jit(solution)/shard_map/ppermute | solution.py:19
  81.5 16.6 %collective-permute-start.12 = (bf16[256,1024]{1,0:T(8,128)(2,1)}, bf16[256,1024]{1,0:T(8,128)(2,1)S(1)}, u32[]{:S(2)}, u32[]{:S(2)}) collective-permute-start(bf16[256,1024]{1,0:T(8,128)(2,1)} %bitcast.12.refs_0_), channel_id=1, source_target_pairs={{0,3},{1,0},{2,1},{3,2},{4,7},{5,4},{6,5},{7,6},{8,11},{9,8},{10,9... | collective-permute-start | bytes 1572872 | tf_op jit(solution)/shard_map/ppermute | solution.py:19
  86.2 22.3 %collective-permute-start.9 = (bf16[256,1024]{1,0:T(8,128)(2,1)S(1)}, bf16[256,1024]{1,0:T(8,128)(2,1)S(1)}, u32[]{:S(2)}, u32[]{:S(2)}) collective-permute-start(bf16[256,1024]{1,0:T(8,128)(2,1)S(1)} %shard_map.113), channel_id=1, source_target_pairs={{0,1},{1,2},{2,3},{3,0},{4,5},{5,6},{6,7},{7,4},{8,9},{9,10},{10,1... | collective-permute-start | bytes 1572872 | tf_op jit(solution)/shard_map/ppermute | solution.py:19
  86.6 21.9 %collective-permute-start.11 = (bf16[256,1024]{1,0:T(8,128)(2,1)S(1)}, bf16[256,1024]{1,0:T(8,128)(2,1)S(1)}, u32[]{:S(2)}, u32[]{:S(2)}) collective-permute-start(bf16[256,1024]{1,0:T(8,128)(2,1)S(1)} %shard_map.114), channel_id=1, source_target_pairs={{0,3},{1,0},{2,1},{3,2},{4,7},{5,4},{6,5},{7,6},{8,11},{9,8},{10,9... | collective-permute-start | bytes 1572872 | tf_op jit(solution)/shard_map/ppermute | solution.py:19
  98.0 24.1 %collective-permute-start.14 = (bf16[128,1024]{1,0:T(8,128)(2,1)}, bf16[128,1024]{1,0:T(8,128)(2,1)}, u32[]{:S(2)}, u32[]{:S(2)}) collective-permute-start(bf16[128,1024]{1,0:T(8,128)(2,1)} %slice.50), channel_id=1, source_target_pairs={{0,1},{1,2},{2,3},{3,0},{4,5},{5,6},{6,7},{7,4},{8,9},{9,10},{10,1... | collective-permute-start | bytes 786440 | tf_op jit(solution)/shard_map/ppermute | solution.py:19
  98.9 23.2 %collective-permute-start.15 = (bf16[128,1024]{1,0:T(8,128)(2,1)}, bf16[128,1024]{1,0:T(8,128)(2,1)}, u32[]{:S(2)}, u32[]{:S(2)}) collective-permute-start(bf16[128,1024]{1,0:T(8,128)(2,1)} %slice.51), channel_id=1, source_target_pairs={{0,3},{1,0},{2,1},{3,2},{4,7},{5,4},{6,5},{7,6},{8,11},{9,8},{10,9... | collective-permute-start | bytes 786440 | tf_op jit(solution)/shard_map/ppermute | solution.py:19
  109.5 58.6 %all-to-all-start.1 = ((bf16[16,16,1152]{2,1,0:T(8,128)(2,1)}), bf16[16,16,1152]{2,1,0:T(8,128)(2,1)}, u32[]{:S(2)}, u32[]{:S(2)}) async-start(bf16[16,16,1152]{2,1,0:T(8,128)(2,1)} %bitcast.9), calls=%async_computation.1 | async-start | bytes 1179648 | tf_op jit(solution)/shard_map/all_to_all | solution.py:23
  137.1 22.9 %collective-permute-start.23 = (bf16[1536,256]{1,0:T(8,128)(2,1)S(1)}, bf16[1536,256]{1,0:T(8,128)(2,1)S(1)}, u32[]{:S(2)}, u32[]{:S(2)}) collective-permute-start(bf16[1536,256]{1,0:T(8,128)(2,1)S(1)} %get-tuple-element.52), channel_id=1, source_target_pairs={{0,4},{4,8},{8,12},{12,0},{1,5},{5,9},{9,13},{13,1},{2,6},{6,10},{... | collective-permute-start | bytes 2359304 | tf_op jit(solution)/shard_map/ppermute | solution.py:19
  137.2 25.1 %collective-permute-start.25 = (bf16[1536,256]{1,0:T(8,128)(2,1)S(1)}, bf16[1536,256]{1,0:T(8,128)(2,1)S(1)}, u32[]{:S(2)}, u32[]{:S(2)}) collective-permute-start(bf16[1536,256]{1,0:T(8,128)(2,1)S(1)} %get-tuple-element.53), channel_id=1, source_target_pairs={{0,12},{4,0},{8,4},{12,8},{1,13},{5,1},{9,5},{13,9},{2,14},{6,2},{... | collective-permute-start | bytes 2359304 | tf_op jit(solution)/shard_map/ppermute | solution.py:19
  148.5 18.6 %collective-permute-start.17 = (bf16[256,1024]{1,0:T(8,128)(2,1)S(1)}, bf16[256,1024]{1,0:T(8,128)(2,1)S(1)}, u32[]{:S(2)}, u32[]{:S(2)}) collective-permute-start(bf16[256,1024]{1,0:T(8,128)(2,1)S(1)} %shard_map.117), channel_id=1, source_target_pairs={{0,1},{1,2},{2,3},{3,0},{4,5},{5,6},{6,7},{7,4},{8,9},{9,10},{10,1... | collective-permute-start | bytes 1572872 | tf_op jit(solution)/shard_map/ppermute | solution.py:19
  148.8 18.3 %collective-permute-start.19 = (bf16[256,1024]{1,0:T(8,128)(2,1)S(1)}, bf16[256,1024]{1,0:T(8,128)(2,1)S(1)}, u32[]{:S(2)}, u32[]{:S(2)}) collective-permute-start(bf16[256,1024]{1,0:T(8,128)(2,1)S(1)} %shard_map.118), channel_id=1, source_target_pairs={{0,3},{1,0},{2,1},{3,2},{4,7},{5,4},{6,5},{7,6},{8,11},{9,8},{10,9... | collective-permute-start | bytes 1572872 | tf_op jit(solution)/shard_map/ppermute | solution.py:19
  162.2 54.9 %collective-permute-start.24 = (bf16[3072,256]{1,0:T(8,128)(2,1)}, bf16[3072,256]{1,0:T(8,128)(2,1)}, u32[]{:S(2)}, u32[]{:S(2)}) collective-permute-start(bf16[3072,256]{1,0:T(8,128)(2,1)} %shard_map.124), channel_id=1, source_target_pairs={{0,4},{4,8},{8,12},{12,0},{1,5},{5,9},{9,13},{13,1},{2,6},{6,10},{... | collective-permute-start | bytes 4718600 | tf_op jit(solution)/shard_map/ppermute | solution.py:19
  164.4 52.7 %collective-permute-start.26 = (bf16[3072,256]{1,0:T(8,128)(2,1)}, bf16[3072,256]{1,0:T(8,128)(2,1)}, u32[]{:S(2)}, u32[]{:S(2)}) collective-permute-start(bf16[3072,256]{1,0:T(8,128)(2,1)} %shard_map.126), channel_id=1, source_target_pairs={{0,12},{4,0},{8,4},{12,8},{1,13},{5,1},{9,5},{13,9},{2,14},{6,2},{... | collective-permute-start | bytes 4718600 | tf_op jit(solution)/shard_map/ppermute | solution.py:19
  168.1 28.1 %all-to-all-start.3 = ((bf16[16,16,1152]{2,1,0:T(8,128)(2,1)}), bf16[16,16,1152]{2,1,0:T(8,128)(2,1)}, u32[]{:S(2)}, u32[]{:S(2)}) async-start(bf16[16,16,1152]{2,1,0:T(8,128)(2,1)} %bitcast.21), calls=%async_computation.3 | async-start | bytes 1179648 | tf_op jit(solution)/shard_map/all_to_all | solution.py:23
  198.8 15.9 %collective-permute-start.22 = (bf16[128,1152]{1,0:T(8,128)(2,1)S(1)}, bf16[128,1152]{1,0:T(8,128)(2,1)S(1)}, u32[]{:S(2)}, u32[]{:S(2)}) collective-permute-start(bf16[128,1152]{1,0:T(8,128)(2,1)S(1)} %shard_map.120.refs_0_), channel_id=1, source_target_pairs={{0,1},{1,2},{2,3},{3,0},{4,5},{5,6},{6,7},{7,4},{8,9},{9,10},{10,1... | collective-permute-start | bytes 884744 | tf_op jit(solution)/shard_map/ppermute | solution.py:19
  (26 other events, 229.8 us)

commit v2 on v1

--- a/solution.py
+++ b/solution.py
@@ -8,10 +8,10 @@
 from jax.sharding import PartitionSpec as P
 
 
-CHUNKS = 2
+CHUNKS = 1
 RING = 4
 LANES = 128
-VMEM_LIMIT = 48 << 20
+MIB = 1 << 20
 
 
 def shift(x, axis, step):
@@ -42,11 +42,11 @@
     return from_prev, from_next
 
 
-def call(kernel, out_shape, **options):
+def call(kernel, out_shape, mib=8, **options):
     return pl.pallas_call(
         kernel,
         out_shape=out_shape,
-        compiler_params=pltpu.CompilerParams(vmem_limit_bytes=VMEM_LIMIT),
+        compiler_params=pltpu.CompilerParams(vmem_limit_bytes=mib * MIB),
         **options,
     )
 
@@ -84,13 +84,29 @@
 def pack(w_gate, w_up, w_down):
     depth, width = w_gate.shape
 
-    def kernel(gate_ref, up_ref, down_ref, out_ref):
-        out_ref[:depth] = gate_ref[...]
-        out_ref[depth : 2 * depth] = up_ref[...]
-        for c in range(depth // width):
-            out_ref[pl.ds(2 * depth + c * width, width)] = down_ref[:, c * width : (c + 1) * width]
-
-    return call(kernel, bf16(3 * depth, width))(w_gate, w_up, w_down)
+    blocks = depth // width
+
+    def kernel(gate_ref, up_ref, down_ref, out_ref, sems):
+        pairs = [(gate_ref, 0, depth), (up_ref, depth, depth)]
+        for c in range(blocks):
+            lanes = down_ref.at[:, pl.ds(c * width, width)]
+            pairs.append((lanes, 2 * depth + c * width, width))
+        copies = [
+            pltpu.make_async_copy(source, out_ref.at[pl.ds(first, count)], sems.at[i])
+            for i, (source, first, count) in enumerate(pairs)
+        ]
+        for copy in copies:
+            copy.start()
+        for copy in copies:
+            copy.wait()
+
+    return call(
+        kernel,
+        bf16(3 * depth, width),
+        in_specs=[pl.BlockSpec(memory_space=pltpu.HBM)] * 3,
+        out_specs=pl.BlockSpec(memory_space=pltpu.VMEM),
+        scratch_shapes=[pltpu.SemaphoreType.DMA((2 + blocks,))],
+    )(w_gate, w_up, w_down)
 
 
 def weight_parts(refs, r, depth):
@@ -142,6 +158,7 @@
     return call(
         kernel,
         (bf16(slots, width), f32(slots, width), f32(slots, width)),
+        mib=14,
         grid_spec=pltpu.PrefetchScalarGridSpec(
             num_scalar_prefetch=1,
             grid=(RING,),
@@ -158,38 +175,24 @@
     )(here, routed_inputs, *weights)
 
 
-def gradients(here, h, scaled, weights, hidden, silu, slope):
+def pair_gradients(here, h, scaled, weights, hidden, silu, slope):
     rows, depth = scaled[0].shape
     width = hidden.shape[1]
     half = depth // 2
     blocks = depth // width
+    places = ((0, 0, rows), (1, 0, rows), (2, 0, rows // 2), (2, rows // 2, rows // 2), (3, 0, rows))
 
     def kernel(here_ref, *refs):
         scaled_refs, weight_refs, refs = refs[:5], refs[5:10], refs[10:]
-        hidden_ref, silu_ref, slope_ref, refs = *refs[:3], refs[3:]
-        pair_ref, extra_ref, own_ref, next_ref, top_ref, bottom_ref, prev_ref, by_r, refs = (
-            *refs[:8],
-            refs[8:],
-        )
-        parts, sems = refs
+        hidden_ref, silu_ref, slope_ref = refs[:3]
+        pair_ref, extra_ref, top_ref, bottom_ref, by_r, sems = refs[3:]
         t = here_ref[1]
-        copies = []
-        for i, (q, first, count) in enumerate(
-            (
-                (0, 0, rows),
-                (1, 0, rows),
-                (2, 0, rows // 2),
-                (2, rows // 2, rows // 2),
-                (3, 0, rows),
+        copies = [
+            pltpu.make_async_copy(
+                scaled_refs[i], by_r.at[(t + q) % RING, pl.ds(first, count)], sems.at[i]
             )
-        ):
-            copies.append(
-                pltpu.make_async_copy(
-                    scaled_refs[i],
-                    by_r.at[(t + q) % RING, pl.ds(first, count)],
-                    sems.at[i],
-                )
-            )
+            for i, (q, first, count) in enumerate(places)
+        ]
         for copy in copies:
             copy.start()
         for copy in copies:
@@ -210,24 +213,15 @@
         lane = lax.broadcasted_iota(jnp.int32, (rows, LANES), 1)
         extra = jnp.where(lane == 0, high, jnp.where(lane == 1, products - high, 0.0))
         extra_ref[...] = extra.astype(jnp.bfloat16)
-        gate_grad = (hidden_grad * slope_ref[...]).astype(jnp.bfloat16)
-        up_grad = (hidden_grad * silu_ref[...]).astype(jnp.bfloat16)
-        pair_ref[:, :width] = gate_grad
-        pair_ref[:, width:] = up_grad
+        pair_ref[:, :width] = (hidden_grad * slope_ref[...]).astype(jnp.bfloat16)
+        pair_ref[:, width:] = (hidden_grad * silu_ref[...]).astype(jnp.bfloat16)
         for r in range(RING):
-            gates, ups, _ = weight_parts(weight_refs, r, depth)
-            q = (r - t + RING) % RING
-            for i in range(2):
-                gate_ref, gate_first = gates[i]
-                up_ref, up_first = ups[i]
-                value = dot(gate_grad, gate_ref[pl.ds(gate_first, half)], 1, 1)
-                value += dot(up_grad, up_ref[pl.ds(up_first, half)], 1, 1)
-                parts[q, :, i * half : (i + 1) * half] = value.astype(jnp.bfloat16)
-        own_ref[...] = parts[0]
-        next_ref[...] = parts[1]
-        top_ref[...] = parts[2, : rows // 2]
-        bottom_ref[...] = parts[2, rows // 2 :]
-        prev_ref[...] = parts[3]
+
+            @pl.when((t + 2) % RING == r)
+            def _():
+                for i, value in enumerate(slot_part(pair_ref, weight_refs, r, depth)):
+                    top_ref[:, i * half : (i + 1) * half] = value[: rows // 2]
+                    bottom_ref[:, i * half : (i + 1) * half] = value[rows // 2 :]
 
     anywhere = pl.BlockSpec(memory_space=pl.ANY)
     whole = pl.BlockSpec(memory_space=pltpu.VMEM)
@@ -237,24 +231,68 @@
         (
             bf16(rows, 2 * width),
             bf16(rows, LANES),
-            bf16(rows, depth),
-            bf16(rows, depth),
             bf16(rows // 2, depth),
             bf16(rows // 2, depth),
-            bf16(rows, depth),
             bf16(RING, rows, depth),
         ),
+        mib=20,
         grid_spec=pltpu.PrefetchScalarGridSpec(
             num_scalar_prefetch=1,
             grid=(1,),
             in_specs=[anywhere] * 5 + [whole] * 5 + [mine] * 3,
-            out_specs=(whole,) * 8,
-            scratch_shapes=[
-                pltpu.VMEM((RING, rows, depth), jnp.bfloat16),
-                pltpu.SemaphoreType.DMA((5,)),
-            ],
+            out_specs=(whole,) * 5,
+            scratch_shapes=[pltpu.SemaphoreType.DMA((5,))],
         ),
     )(here, *scaled, *weights, hidden, silu, slope)
+
+
+def slot_part(pair_ref, weight_refs, r, depth):
+    half = depth // 2
+    width = pair_ref.shape[1] // 2
+    gates, ups, _ = weight_parts(weight_refs, r, depth)
+    values = []
+    for i in range(2):
+        gate_ref, gate_first = gates[i]
+        up_ref, up_first = ups[i]
+        value = dot(pair_ref[:, :width], gate_ref[pl.ds(gate_first, half)], 1, 1)
+        value += dot(pair_ref[:, width:], up_ref[pl.ds(up_first, half)], 1, 1)
+        values.append(value.astype(jnp.bfloat16))
+    return values
+
+
+def slot_gradients(here, pair, weights):
+    rows = pair.shape[0]
+    depth = weights[0].shape[0] // 3
+    half = depth // 2
+
+    def kernel(here_ref, pair_ref, *refs):
+        weight_refs, (own_ref, next_ref, prev_ref, parts) = refs[:5], refs[5:]
+        t = here_ref[1]
+        for r in range(RING):
+            q = (r - t + RING) % RING
+
+            @pl.when(q != 2)
+            def _():
+                for i, value in enumerate(slot_part(pair_ref, weight_refs, r, depth)):
+                    parts[q, :, i * half : (i + 1) * half] = value
+
+        own_ref[...] = parts[0]
+        next_ref[...] = parts[1]
+        prev_ref[...] = parts[3]
+
+    whole = pl.BlockSpec(memory_space=pltpu.VMEM)
+    return call(
+        kernel,
+        (bf16(rows, depth),) * 3,
+        mib=16,
+        grid_spec=pltpu.PrefetchScalarGridSpec(
+            num_scalar_prefetch=1,
+            grid=(1,),
+            in_specs=[whole] * 6,
+            out_specs=(whole,) * 3,
+            scratch_shapes=[pltpu.VMEM((RING, rows, depth), jnp.bfloat16)],
+        ),
+    )(here, pair, *weights)
 
 
 def weight_chunk(here, r, routed_inputs, hidden, pairs, scaled, received=None):
@@ -319,6 +357,7 @@
     return call(
         kernel,
         outs,
+        mib=16 if r == 0 else 10,
         grid_spec=pltpu.PrefetchScalarGridSpec(
             num_scalar_prefetch=1,
             grid=(1,),
@@ -454,9 +493,10 @@
     hidden, silu, slope = activations(here, routed_inputs, weights, width)
     pairs, scaled, back = [], [], []
     for h in range(CHUNKS):
-        pair, extra, own, following, top, bottom, prev, by_r = gradients(
+        pair, extra, top, bottom, by_r = pair_gradients(
             here, h, arrived[h], weights, hidden, silu, slope
         )
+        own, following, prev = slot_gradients(here, pair, weights)
         pairs.append(pair)
         scaled.append(by_r)
         received = ring_reduce(following, top, bottom, prev, "tp")

time: 223 us -> 222 us (level)
  waiting for transfers between devices: 68.2 us -> 125 us
  blocking collectives: 26.5 us -> 0 us
  starting transfers between devices: 62.1 us -> 43.4 us
  Pallas kernels: 48.8 us -> 34.9 us
  other arithmetic: 2.07 us -> 4.67 us
    ppermute x27 -> x19, waiting for transfers between devices: 49.7 us -> 99.5 us  [shift(): return lax.ppermute(x, axis, [(i, (i + step) % n) for i in range(n)])]
    all_to_all x1 -> x0, blocking collectives: 26.5 us -> none  [exchange(): return lax.all_to_all(x, 'ep', split_axis=0, concat_axis=0, tiled=True)]
    pallas_call x7, Pallas kernels: 32.7 us -> 20.7 us  [the longest x4 10.6 us: weight_chunk(): call(kernel, outs, mib=16 if r == 0 else 10, grid_spec=pltpu.PrefetchScal...]
    all_to_all x3 -> x2, starting transfers between devices: 26.2 us -> 16.7 us  [exchange(): return lax.all_to_all(x, 'ep', split_axis=0, concat_axis=0, tiled=True)]
    ppermute x27 -> x19, starting transfers between devices: 35.9 us -> 26.7 us  [shift(): return lax.ppermute(x, axis, [(i, (i + step) % n) for i in range(n)])]
    all_to_all x3 -> x2, waiting for transfers between devices: 18.5 us -> 25.1 us  [exchange(): return lax.all_to_all(x, 'ep', split_axis=0, concat_axis=0, tiled=True)]
    pallas_call x6 -> x4, Pallas kernels: 5.28 us -> 3.72 us  [add_half(): call(kernel, bf16(*whole.shape), grid=(1,), in_specs=[spec, pl.BlockSpec(...]
    unnamed x41 -> x23, local copies, waits for them, and re-layouts: 7.87 us -> 9.42 us
  transfers between devices with their start and end apart: 30 -> 21, of which waited for: 11 -> 12; matrix products, arithmetic and copies ran while one was open for 4% -> 1% of each run, Pallas kernels for 20% -> 12%
where the time goes in v2:
time: 222 us; the launch traced here: 221 us
  waiting for transfers between devices  125 us (56%)
  starting transfers between devices  43.4 us (20%)
  Pallas kernels  34.9 us (16%)
  local copies, waits for them, and re-layouts  11.2 us (5%)
  other arithmetic  4.67 us (2%)
    ppermute x19, waiting for transfers between devices, shift(): return lax.ppermute(x, axis, [(i, (i + step) % n) for i in range(n)])  99.5 us
    ppermute x19, starting transfers between devices, shift(): return lax.ppermute(x, axis, [(i, (i + step) % n) for i in range(n)])  26.7 us
    all_to_all x2, waiting for transfers between devices, exchange(): return lax.all_to_all(x, 'ep', split_axis=0, concat_axis=0, tiled=True)  25.1 us
    all_to_all x2, starting transfers between devices, exchange(): return lax.all_to_all(x, 'ep', split_axis=0, concat_axis=0, tiled=True)  16.7 us
    pallas_call x4, Pallas kernels, weight_chunk(): call(kernel, outs, mib=16 if r == 0 else 10, grid_spec=pltpu.PrefetchScal...  10.6 us
    unnamed x23, local copies, waits for them, and re-layouts  9.42 us
    pallas_call x1, Pallas kernels, pair_gradients(): call(kernel, (bf16(rows, 2 * width), bf16(rows, LANES), bf16(rows // 2, d...  5.54 us
    pallas_call x1, Pallas kernels, activations(): call(kernel, (bf16(slots, width), f32(slots, width), f32(slots, width)),...  5.28 us
  transfers between devices with their start and end apart: 21, of which 12 were waited for; matrix products, arithmetic and copies ran while one was open for 1% of the time, Pallas kernels for 12%

profile of v2, /device:TPU:1, one launch (start us, length us, event | category | flops | bytes accessed | tf_op | source)
XLA Modules:
  0.0 221.3 jit_solution(6024407406716259876)
XLA Ops:
  7.1 10.0 %all-to-all-start = ((bf16[16,32,1024]{2,1,0:T(8,128)(2,1)}), bf16[16,32,1024]{2,1,0:T(8,128)(2,1)}, u32[]{:S(2)}, u32[]{:S(2)}) async-start(bf16[16,32,1024]{2,1,0:T(8,128)(2,1)} %bitcast.4), calls=%async_computation | async-start | bytes 2097152 | tf_op jit(solution)/shard_map/all_to_all | solution.py:23
  20.1 25.1 %all-to-all-done = bf16[16,32,1024]{2,1,0:T(8,128)(2,1)} async-done(((bf16[16,32,1024]{2,1,0:T(8,128)(2,1)}), bf16[16,32,1024]{2,1,0:T(8,128)(2,1)}, u32[]{:S(2)}, u32[]{:S(2)}) %all-to-all-start) | async-done | bytes 1048608 | tf_op jit(solution)/shard_map/all_to_all | solution.py:23
  47.9 6.5 %collective-permute-done.5.w4.refs_9_.refs_4_ = bf16[3072,256]{1,0:T(8,128)(2,1)S(1)} collective-permute-done((bf16[3072,256]{1,0:T(8,128)(2,1)S(1)}, bf16[3072,256]{1,0:T(8,128)(2,1)S(1)}, u32[]{:S(2)}, u32[]{:S(2)}) %collective-permute-start.5) | collective-permute-done | bytes 1572896 | tf_op jit(solution)/shard_map/ppermute | solution.py:19
  56.0 2.5 %collective-permute-start.7 = (bf16[1536,256]{1,0:T(8,128)(2,1)S(1)}, bf16[1536,256]{1,0:T(8,128)(2,1)S(1)}, u32[]{:S(2)}, u32[]{:S(2)}) collective-permute-start(bf16[1536,256]{1,0:T(8,128)(2,1)S(1)} %slice.29), channel_id=1, source_target_pairs={{0,12},{4,0},{8,4},{12,8},{1,13},{5,1},{9,5},{13,9},{2,14},{6,2},{... | collective-permute-start | bytes 2359304 | tf_op jit(solution)/shard_map/ppermute | solution.py:19
  58.5 12.3 %collective-permute-done.1.refs_4_ = bf16[512,1024]{1,0:T(8,128)(2,1)S(1)} collective-permute-done((bf16[512,1024]{1,0:T(8,128)(2,1)}, bf16[512,1024]{1,0:T(8,128)(2,1)S(1)}, u32[]{:S(2)}, u32[]{:S(2)}) %collective-permute-start.1) | collective-permute-done | bytes 1048608 | tf_op jit(solution)/shard_map/ppermute | solution.py:19
  71.2 2.7 %collective-permute-start.3 = (bf16[256,1024]{1,0:T(8,128)(2,1)S(1)}, bf16[256,1024]{1,0:T(8,128)(2,1)S(1)}, u32[]{:S(2)}, u32[]{:S(2)}) collective-permute-start(bf16[256,1024]{1,0:T(8,128)(2,1)S(1)} %slice.27), channel_id=1, source_target_pairs={{0,3},{1,0},{2,1},{3,2},{4,7},{5,4},{6,5},{7,6},{8,11},{9,8},{10,9... | collective-permute-start | bytes 1572872 | tf_op jit(solution)/shard_map/ppermute | solution.py:19
  74.1 5.3 %shard_map.111 = (bf16[512,256]{1,0:T(8,128)(2,1)S(1)}, f32[512,256]{1,0:T(8,128)S(1)}, f32[512,256]{1,0:T(8,128)S(1)}) custom-call(s32[2]{0:T(128)S(1)} %pad_add_fusion.here_ref, bf16[1,16,1,32,4096]{4,3,2,1,0:T(8,128)(2,1)S(1)} %copy-done, bf16[3072,256]{1,0:T(8,128)(2,1)S(1)} %shard_map.110.w0.refs_5_.refs_0_, ...), custom_call_target="tpu_custom_call" | custom-call | tf_op jit(solution)/shard_map/pallas_call | solution.py:158
  79.4 6.4 %collective-permute-done.2.refs_2_ = bf16[256,1024]{1,0:T(8,128)(2,1)S(1)} collective-permute-done((bf16[256,1024]{1,0:T(8,128)(2,1)S(1)}, bf16[256,1024]{1,0:T(8,128)(2,1)S(1)}, u32[]{:S(2)}, u32[]{:S(2)}) %collective-permute-start.2) | collective-permute-done | bytes 524320 | tf_op jit(solution)/shard_map/ppermute | solution.py:19
  85.8 5.5 %shard_map.112 = (bf16[512,512]{1,0:T(8,128)(2,1)S(1)}, bf16[512,128]{1,0:T(8,128)(2,1)S(1)}, bf16[256,1024]{1,0:T(8,128)(2,1)S(1)}, bf16[256,1024]{1,0:T(8,128)(2,1)S(1)}, bf16[4,512,1024]{2,1,0:T(8,128)(2,1)S(1)}) custom-call(s32[2]{0:T(128)S(1)} %pad_add_fusion.here_ref, bf16[512,1024]{1,0:T(8,128)(2,1)} %bitcast.5.refs_0_, ...), custom_call_target="tpu_custom_call" | custom-call | tf_op jit(solution)/shard_map/pallas_call | solution.py:229
  91.4 3.2 %collective-permute-start.10 = (bf16[256,1024]{1,0:T(8,128)(2,1)S(1)}, bf16[256,1024]{1,0:T(8,128)(2,1)S(1)}, u32[]{:S(2)}, u32[]{:S(2)}) collective-permute-start(bf16[256,1024]{1,0:T(8,128)(2,1)S(1)} %get-tuple-element.31), channel_id=1, source_target_pairs={{0,3},{1,0},{2,1},{3,2},{4,7},{5,4},{6,5},{7,6},{8,11},{9,8},{10,9... | collective-permute-start | bytes 1572872 | tf_op jit(solution)/shard_map/ppermute | solution.py:19
  94.6 4.4 %shard_map.113 = (bf16[512,1024]{1,0:T(8,128)(2,1)S(1)}, bf16[512,1024]{1,0:T(8,128)(2,1)S(1)}, bf16[512,1024]{1,0:T(8,128)(2,1)S(1)}) custom-call(s32[2]{0:T(128)S(1)} %pad_add_fusion.here_ref, bf16[512,512]{1,0:T(8,128)(2,1)S(1)} %get-tuple-element.26.pair_ref.refs_0_, bf16[3072,256]{1,0:T(8,128)(2,1)S(1)} %shard_map.110.w0.refs_5_.refs_0_, ...), custom_call_target="tpu_custom_call" | custom-call | tf_op jit(solution)/shard_map/pallas_call | solution.py:284
  99.0 6.3 %collective-permute-done.10.half_ref = bf16[256,1024]{1,0:T(8,128)(2,1)S(1)} collective-permute-done((bf16[256,1024]{1,0:T(8,128)(2,1)S(1)}, bf16[256,1024]{1,0:T(8,128)(2,1)S(1)}, u32[]{:S(2)}, u32[]{:S(2)}) %collective-permute-start.10) | collective-permute-done | bytes 524320 | tf_op jit(solution)/shard_map/ppermute | solution.py:19
  105.7 3.5 %collective-permute-start.11 = (bf16[512,1024]{1,0:T(8,128)(2,1)S(1)}, bf16[512,1024]{1,0:T(8,128)(2,1)S(1)}, u32[]{:S(2)}, u32[]{:S(2)}) collective-permute-start(bf16[512,1024]{1,0:T(8,128)(2,1)S(1)} %shard_map.115), channel_id=1, source_target_pairs={{0,3},{1,0},{2,1},{3,2},{4,7},{5,4},{6,5},{7,6},{8,11},{9,8},{10,9... | collective-permute-start | bytes 3145736 | tf_op jit(solution)/shard_map/ppermute | solution.py:19
  109.7 20.6 %collective-permute-done.11.next_ref = bf16[512,1024]{1,0:T(8,128)(2,1)S(1)} collective-permute-done((bf16[512,1024]{1,0:T(8,128)(2,1)S(1)}, bf16[512,1024]{1,0:T(8,128)(2,1)S(1)}, u32[]{:S(2)}, u32[]{:S(2)}) %collective-permute-start.11) | collective-permute-done | bytes 1048608 | tf_op jit(solution)/shard_map/ppermute | solution.py:19
  130.4 3.6 %collective-permute-done.9.prev_ref = bf16[512,1024]{1,0:T(8,128)(2,1)S(1)} collective-permute-done((bf16[512,1024]{1,0:T(8,128)(2,1)S(1)}, bf16[512,1024]{1,0:T(8,128)(2,1)S(1)}, u32[]{:S(2)}, u32[]{:S(2)}) %collective-permute-start.9) | collective-permute-done | bytes 1048608 | tf_op jit(solution)/shard_map/ppermute | solution.py:19
  135.4 6.8 %all-to-all-start.1 = ((bf16[16,32,1152]{2,1,0:T(8,128)(2,1)}), bf16[16,32,1152]{2,1,0:T(8,128)(2,1)}, u32[]{:S(2)}, u32[]{:S(2)}) async-start(bf16[16,32,1152]{2,1,0:T(8,128)(2,1)} %bitcast.9), calls=%async_computation.1 | async-start | bytes 2359296 | tf_op jit(solution)/shard_map/all_to_all | solution.py:23
  148.2 2.6 %collective-permute-start.17 = (bf16[1536,256]{1,0:T(8,128)(2,1)S(1)}, bf16[1536,256]{1,0:T(8,128)(2,1)S(1)}, u32[]{:S(2)}, u32[]{:S(2)}) collective-permute-start(bf16[1536,256]{1,0:T(8,128)(2,1)S(1)} %get-tuple-element.37), channel_id=1, source_target_pairs={{0,12},{4,0},{8,4},{12,8},{1,13},{5,1},{9,5},{13,9},{2,14},{6,2},{... | collective-permute-start | bytes 2359304 | tf_op jit(solution)/shard_map/ppermute | solution.py:19
  150.7 2.8 %shard_map.122.whole_ref = bf16[3072,256]{1,0:T(8,128)(2,1)} custom-call(s32[2]{0:T(128)S(1)} %pad_add_fusion.here_ref, bf16[1,16,1,32,4096]{4,3,2,1,0:T(8,128)(2,1)S(1)} %copy-done.1, bf16[512,256]{1,0:T(8,128)(2,1)S(1)} %get-tuple-element.23.refs_10_.hidden_ref, bf16[512,512]{1,0:T(8,128)(2,1)S(1)} %copy-done.7, bf16[4,512,1024]{2,1,0:T(8,128)(2,1)S(1)} %copy-done.4), custom_call_target="tpu_custom_call" | custom-call | tf_op jit(solution)/shard_map/pallas_call | solution.py:357
  155.2 12.2 %collective-permute-done.17.half_ref = bf16[1536,256]{1,0:T(8,128)(2,1)S(1)} collective-permute-done((bf16[1536,256]{1,0:T(8,128)(2,1)S(1)}, bf16[1536,256]{1,0:T(8,128)(2,1)S(1)}, u32[]{:S(2)}, u32[]{:S(2)}) %collective-permute-start.17) | collective-permute-done | bytes 786464 | tf_op jit(solution)/shard_map/ppermute | solution.py:19
  167.3 2.3 %shard_map.123 = bf16[3072,256]{1,0:T(8,128)(2,1)} custom-call(bf16[3072,256]{1,0:T(8,128)(2,1)} %shard_map.122.whole_ref, bf16[1536,256]{1,0:T(8,128)(2,1)S(1)} %collective-permute-done.17.half_ref), custom_call_target="tpu_custom_call", output_to_operand_aliasing={{}: (0, {})} | custom-call | tf_op jit(solution)/shard_map/pallas_call | solution.py:74
  169.6 3.5 %collective-permute-start.18 = (bf16[3072,256]{1,0:T(8,128)(2,1)}, bf16[3072,256]{1,0:T(8,128)(2,1)}, u32[]{:S(2)}, u32[]{:S(2)}) collective-permute-start(bf16[3072,256]{1,0:T(8,128)(2,1)} %shard_map.123), channel_id=1, source_target_pairs={{0,12},{4,0},{8,4},{12,8},{1,13},{5,1},{9,5},{13,9},{2,14},{6,2},{... | collective-permute-start | bytes 4718600 | tf_op jit(solution)/shard_map/ppermute | solution.py:19
  178.6 27.6 %collective-permute-done.18.refs_3_ = bf16[3072,256]{1,0:T(8,128)(2,1)} collective-permute-done((bf16[3072,256]{1,0:T(8,128)(2,1)}, bf16[3072,256]{1,0:T(8,128)(2,1)}, u32[]{:S(2)}, u32[]{:S(2)}) %collective-permute-start.18) | collective-permute-done | bytes 1572896 | tf_op jit(solution)/shard_map/ppermute | solution.py:19
  206.2 3.6 %collective-permute-done.16.refs_2_ = bf16[3072,256]{1,0:T(8,128)(2,1)} collective-permute-done((bf16[3072,256]{1,0:T(8,128)(2,1)S(1)}, bf16[3072,256]{1,0:T(8,128)(2,1)}, u32[]{:S(2)}, u32[]{:S(2)}) %collective-permute-start.16) | collective-permute-done | bytes 1572896 | tf_op jit(solution)/shard_map/ppermute | solution.py:19
  214.2 4.6 %shard_map.124 = (f32[1024,256]{1,0:T(8,128)}, f32[1024,256]{1,0:T(8,128)}, f32[256,1024]{1,0:T(8,128)}) custom-call(s32[2]{0:T(128)S(1)} %pad_add_fusion.here_ref, bf16[1,16,1,32,4096]{4,3,2,1,0:T(8,128)(2,1)S(1)} %copy-done.2, bf16[512,256]{1,0:T(8,128)(2,1)S(1)} %get-tuple-element.23.refs_10_.hidden_ref, bf16[512,512]{1,0:T(8,128)(2,1)S(1)} %copy-done.7, ...), custom_call_target="tpu_custom_call" | custom-call | tf_op jit(solution)/shard_map/pallas_call | solution.py:357
  (73 shorter events, 36.5 us)
Async XLA Ops:
  5.6 11.5 %copy-start.8 = (bf16[1,1024,256]{2,1,0:T(8,128)(2,1)S(1)}, bf16[1,1024,256]{2,1,0:T(8,128)(2,1)}, u32[]{:S(2)}) copy-start(bf16[1,1024,256]{2,1,0:T(8,128)(2,1)} %param.11) | copy-start | bytes 1572868
  5.6 11.5 %copy-start.9 = (bf16[1,1024,256]{2,1,0:T(8,128)(2,1)S(1)}, bf16[1,1024,256]{2,1,0:T(8,128)(2,1)}, u32[]{:S(2)}) copy-start(bf16[1,1024,256]{2,1,0:T(8,128)(2,1)} %param.12) | copy-start | bytes 1572868
  7.1 38.1 %all-to-all-start = ((bf16[16,32,1024]{2,1,0:T(8,128)(2,1)}), bf16[16,32,1024]{2,1,0:T(8,128)(2,1)}, u32[]{:S(2)}, u32[]{:S(2)}) async-start(bf16[16,32,1024]{2,1,0:T(8,128)(2,1)} %bitcast.4), calls=%async_computation | async-start | bytes 2097152 | tf_op jit(solution)/shard_map/all_to_all | solution.py:23
  17.3 37.1 %collective-permute-start.5 = (bf16[3072,256]{1,0:T(8,128)(2,1)S(1)}, bf16[3072,256]{1,0:T(8,128)(2,1)S(1)}, u32[]{:S(2)}, u32[]{:S(2)}) collective-permute-start(bf16[3072,256]{1,0:T(8,128)(2,1)S(1)} %shard_map.110.w0.refs_5_.refs_0_), channel_id=1, source_target_pairs={{0,4},{4,8},{8,12},{12,0},{1,5},{5,9},{9,13},{13,1},{2,6},{6,10},{... | collective-permute-start | bytes 4718600 | tf_op jit(solution)/shard_map/ppermute | solution.py:19
  18.6 36.0 %collective-permute-start.4 = (bf16[3072,256]{1,0:T(8,128)(2,1)S(1)}, bf16[3072,256]{1,0:T(8,128)(2,1)}, u32[]{:S(2)}, u32[]{:S(2)}) collective-permute-start(bf16[3072,256]{1,0:T(8,128)(2,1)S(1)} %shard_map.110.w0.refs_5_.refs_0_), channel_id=1, source_target_pairs={{0,12},{4,0},{8,4},{12,8},{1,13},{5,1},{9,5},{13,9},{2,14},{6,2},{... | collective-permute-start | bytes 4718600 | tf_op jit(solution)/shard_map/ppermute | solution.py:19
  45.2 25.7 %collective-permute-start.1 = (bf16[512,1024]{1,0:T(8,128)(2,1)}, bf16[512,1024]{1,0:T(8,128)(2,1)S(1)}, u32[]{:S(2)}, u32[]{:S(2)}) collective-permute-start(bf16[512,1024]{1,0:T(8,128)(2,1)} %bitcast.5.refs_0_), channel_id=1, source_target_pairs={{0,1},{1,2},{2,3},{3,0},{4,5},{5,6},{6,7},{7,4},{8,9},{9,10},{10,1... | collective-permute-start | bytes 3145736 | tf_op jit(solution)/shard_map/ppermute | solution.py:19
  46.5 24.7 %collective-permute-start = (bf16[512,1024]{1,0:T(8,128)(2,1)}, bf16[512,1024]{1,0:T(8,128)(2,1)S(1)}, u32[]{:S(2)}, u32[]{:S(2)}) collective-permute-start(bf16[512,1024]{1,0:T(8,128)(2,1)} %bitcast.5.refs_0_), channel_id=1, source_target_pairs={{0,3},{1,0},{2,1},{3,2},{4,7},{5,4},{6,5},{7,6},{8,11},{9,8},{10,9... | collective-permute-start | bytes 3145736 | tf_op jit(solution)/shard_map/ppermute | solution.py:19
  54.4 19.7 %copy-start = (bf16[1,16,1,32,4096]{4,3,2,1,0:T(8,128)(2,1)S(1)}, bf16[1,16,1,32,4096]{4,3,2,1,0:T(8,128)(2,1)}, u32[]{:S(2)}) copy-start(bf16[1,16,1,32,4096]{4,3,2,1,0:T(8,128)(2,1)} %x_ref.9) | copy-start | bytes 12582916
  54.5 19.5 %collective-permute-start.6 = (bf16[1536,256]{1,0:T(8,128)(2,1)S(1)}, bf16[1536,256]{1,0:T(8,128)(2,1)S(1)}, u32[]{:S(2)}, u32[]{:S(2)}) collective-permute-start(bf16[1536,256]{1,0:T(8,128)(2,1)S(1)} %slice.28), channel_id=1, source_target_pairs={{0,4},{4,8},{8,12},{12,0},{1,5},{5,9},{9,13},{13,1},{2,6},{6,10},{... | collective-permute-start | bytes 2359304 | tf_op jit(solution)/shard_map/ppermute | solution.py:19
  56.0 18.1 %collective-permute-start.7 = (bf16[1536,256]{1,0:T(8,128)(2,1)S(1)}, bf16[1536,256]{1,0:T(8,128)(2,1)S(1)}, u32[]{:S(2)}, u32[]{:S(2)}) collective-permute-start(bf16[1536,256]{1,0:T(8,128)(2,1)S(1)} %slice.29), channel_id=1, source_target_pairs={{0,12},{4,0},{8,4},{12,8},{1,13},{5,1},{9,5},{13,9},{2,14},{6,2},{... | collective-permute-start | bytes 2359304 | tf_op jit(solution)/shard_map/ppermute | solution.py:19
  70.9 14.9 %collective-permute-start.2 = (bf16[256,1024]{1,0:T(8,128)(2,1)S(1)}, bf16[256,1024]{1,0:T(8,128)(2,1)S(1)}, u32[]{:S(2)}, u32[]{:S(2)}) collective-permute-start(bf16[256,1024]{1,0:T(8,128)(2,1)S(1)} %slice.26), channel_id=1, source_target_pairs={{0,1},{1,2},{2,3},{3,0},{4,5},{5,6},{6,7},{7,4},{8,9},{9,10},{10,1... | collective-permute-start | bytes 1572872 | tf_op jit(solution)/shard_map/ppermute | solution.py:19
  71.2 14.5 %collective-permute-start.3 = (bf16[256,1024]{1,0:T(8,128)(2,1)S(1)}, bf16[256,1024]{1,0:T(8,128)(2,1)S(1)}, u32[]{:S(2)}, u32[]{:S(2)}) collective-permute-start(bf16[256,1024]{1,0:T(8,128)(2,1)S(1)} %slice.27), channel_id=1, source_target_pairs={{0,3},{1,0},{2,1},{3,2},{4,7},{5,4},{6,5},{7,6},{8,11},{9,8},{10,9... | collective-permute-start | bytes 1572872 | tf_op jit(solution)/shard_map/ppermute | solution.py:19
  91.4 14.0 %collective-permute-start.10 = (bf16[256,1024]{1,0:T(8,128)(2,1)S(1)}, bf16[256,1024]{1,0:T(8,128)(2,1)S(1)}, u32[]{:S(2)}, u32[]{:S(2)}) collective-permute-start(bf16[256,1024]{1,0:T(8,128)(2,1)S(1)} %get-tuple-element.31), channel_id=1, source_target_pairs={{0,3},{1,0},{2,1},{3,2},{4,7},{5,4},{6,5},{7,6},{8,11},{9,8},{10,9... | collective-permute-start | bytes 1572872 | tf_op jit(solution)/shard_map/ppermute | solution.py:19
  94.6 14.7 %collective-permute-start.8 = (bf16[256,1024]{1,0:T(8,128)(2,1)S(1)}, bf16[256,1024]{1,0:T(8,128)(2,1)S(1)}, u32[]{:S(2)}, u32[]{:S(2)}) collective-permute-start(bf16[256,1024]{1,0:T(8,128)(2,1)S(1)} %get-tuple-element.29), channel_id=1, source_target_pairs={{0,1},{1,2},{2,3},{3,0},{4,5},{5,6},{6,7},{7,4},{8,9},{9,10},{10,1... | collective-permute-start | bytes 1572872 | tf_op jit(solution)/shard_map/ppermute | solution.py:19
  105.7 24.6 %collective-permute-start.11 = (bf16[512,1024]{1,0:T(8,128)(2,1)S(1)}, bf16[512,1024]{1,0:T(8,128)(2,1)S(1)}, u32[]{:S(2)}, u32[]{:S(2)}) collective-permute-start(bf16[512,1024]{1,0:T(8,128)(2,1)S(1)} %shard_map.115), channel_id=1, source_target_pairs={{0,3},{1,0},{2,1},{3,2},{4,7},{5,4},{6,5},{7,6},{8,11},{9,8},{10,9... | collective-permute-start | bytes 3145736 | tf_op jit(solution)/shard_map/ppermute | solution.py:19
  109.6 24.3 %collective-permute-start.9 = (bf16[512,1024]{1,0:T(8,128)(2,1)S(1)}, bf16[512,1024]{1,0:T(8,128)(2,1)S(1)}, u32[]{:S(2)}, u32[]{:S(2)}) collective-permute-start(bf16[512,1024]{1,0:T(8,128)(2,1)S(1)} %shard_map.114), channel_id=1, source_target_pairs={{0,1},{1,2},{2,3},{3,0},{4,5},{5,6},{6,7},{7,4},{8,9},{9,10},{10,1... | collective-permute-start | bytes 3145736 | tf_op jit(solution)/shard_map/ppermute | solution.py:19
  135.4 38.6 %all-to-all-start.1 = ((bf16[16,32,1152]{2,1,0:T(8,128)(2,1)}), bf16[16,32,1152]{2,1,0:T(8,128)(2,1)}, u32[]{:S(2)}, u32[]{:S(2)}) async-start(bf16[16,32,1152]{2,1,0:T(8,128)(2,1)} %bitcast.9), calls=%async_computation.1 | async-start | bytes 2359296 | tf_op jit(solution)/shard_map/all_to_all | solution.py:23
  148.2 19.2 %collective-permute-start.17 = (bf16[1536,256]{1,0:T(8,128)(2,1)S(1)}, bf16[1536,256]{1,0:T(8,128)(2,1)S(1)}, u32[]{:S(2)}, u32[]{:S(2)}) collective-permute-start(bf16[1536,256]{1,0:T(8,128)(2,1)S(1)} %get-tuple-element.37), channel_id=1, source_target_pairs={{0,12},{4,0},{8,4},{12,8},{1,13},{5,1},{9,5},{13,9},{2,14},{6,2},{... | collective-permute-start | bytes 2359304 | tf_op jit(solution)/shard_map/ppermute | solution.py:19
  150.7 22.4 %collective-permute-start.15 = (bf16[1536,256]{1,0:T(8,128)(2,1)S(1)}, bf16[1536,256]{1,0:T(8,128)(2,1)S(1)}, u32[]{:S(2)}, u32[]{:S(2)}) collective-permute-start(bf16[1536,256]{1,0:T(8,128)(2,1)S(1)} %get-tuple-element.36), channel_id=1, source_target_pairs={{0,4},{4,8},{8,12},{12,0},{1,5},{5,9},{9,13},{13,1},{2,6},{6,10},{... | collective-permute-start | bytes 2359304 | tf_op jit(solution)/shard_map/ppermute | solution.py:19
  169.6 36.6 %collective-permute-start.18 = (bf16[3072,256]{1,0:T(8,128)(2,1)}, bf16[3072,256]{1,0:T(8,128)(2,1)}, u32[]{:S(2)}, u32[]{:S(2)}) collective-permute-start(bf16[3072,256]{1,0:T(8,128)(2,1)} %shard_map.123), channel_id=1, source_target_pairs={{0,12},{4,0},{8,4},{12,8},{1,13},{5,1},{9,5},{13,9},{2,14},{6,2},{... | collective-permute-start | bytes 4718600 | tf_op jit(solution)/shard_map/ppermute | solution.py:19
  173.8 36.0 %collective-permute-start.16 = (bf16[3072,256]{1,0:T(8,128)(2,1)S(1)}, bf16[3072,256]{1,0:T(8,128)(2,1)}, u32[]{:S(2)}, u32[]{:S(2)}) collective-permute-start(bf16[3072,256]{1,0:T(8,128)(2,1)S(1)} %shard_map.121), channel_id=1, source_target_pairs={{0,4},{4,8},{8,12},{12,0},{1,5},{5,9},{9,13},{13,1},{2,6},{6,10},{... | collective-permute-start | bytes 4718600 | tf_op jit(solution)/shard_map/ppermute | solution.py:19
  175.9 42.9 %collective-permute-start.14 = (bf16[128,1152]{1,0:T(8,128)(2,1)S(1)}, bf16[128,1152]{1,0:T(8,128)(2,1)S(1)}, u32[]{:S(2)}, u32[]{:S(2)}) collective-permute-start(bf16[128,1152]{1,0:T(8,128)(2,1)S(1)} %shard_map.117.refs_0_), channel_id=1, source_target_pairs={{0,1},{1,2},{2,3},{3,0},{4,5},{5,6},{6,7},{7,4},{8,9},{9,10},{10,1... | collective-permute-start | bytes 884744 | tf_op jit(solution)/shard_map/ppermute | solution.py:19
  176.0 42.8 %collective-permute-start.13 = (bf16[128,1152]{1,0:T(8,128)(2,1)S(1)}, bf16[128,1152]{1,0:T(8,128)(2,1)S(1)}, u32[]{:S(2)}, u32[]{:S(2)}) collective-permute-start(bf16[128,1152]{1,0:T(8,128)(2,1)S(1)} %shard_map.117.refs_0_), channel_id=1, source_target_pairs={{0,2},{1,3},{2,0},{3,1},{4,6},{5,7},{6,4},{7,5},{8,10},{9,11},{10,... | collective-permute-start | bytes 884744 | tf_op jit(solution)/shard_map/ppermute | solution.py:19
  176.6 42.1 %collective-permute-start.12 = (bf16[128,1152]{1,0:T(8,128)(2,1)S(1)}, bf16[128,1152]{1,0:T(8,128)(2,1)S(1)}, u32[]{:S(2)}, u32[]{:S(2)}) collective-permute-start(bf16[128,1152]{1,0:T(8,128)(2,1)S(1)} %shard_map.117.refs_0_), channel_id=1, source_target_pairs={{0,3},{1,0},{2,1},{3,2},{4,7},{5,4},{6,5},{7,6},{8,11},{9,8},{10,9... | collective-permute-start | bytes 884744 | tf_op jit(solution)/shard_map/ppermute | solution.py:19
  (8 other events, 42.3 us)
